TPU v7x, 16 devices: a whole 2x2x2 slice. The times are simulated.
16 devices in a mesh: pod: 4 (over z, y), data: 4 (over x, core).
Axes of the slice: x: 2, y: 2, z: 2, core: 2. Of those that a mesh axis runs over, the one named last changes fastest.
Arguments:
- w_first: float32 [16, 256, 1024], replicated
- w_second: float32 [16, 1024, 256], replicated
- m_first: float32 [16, 256, 1024], replicated
- m_second: float32 [16, 1024, 256], replicated
- x_now: bfloat16 [16384, 256], P(('pod', 'data'))
- y_now: bfloat16 [16384, 256], P(('pod', 'data'))
- x_next: bfloat16 [16384, 256], P(('pod', 'data'))
- y_next: bfloat16 [16384, 256], P(('pod', 'data'))
Outputs:
- output 1: float32 [16, 256, 1024], replicated
- output 2: float32 [16, 1024, 256], replicated
- output 3: float32 [16, 256, 1024], replicated
- output 4: float32 [16, 1024, 256], replicated
- output 5: float32 [16384], P(('pod', 'data'))
- output 6: float32 [16384, 256], P(('pod', 'data'))
All inputs are finite; a program needn't handle non-finite values.
Results may differ from a plain program's by a relative error of at most 0.011314.
Values are sent between devices in bfloat16 or wider.
A program may use at most 1 GiB of HBM per device.

v0:
```python
import jax
import jax.numpy as jnp
from jax import lax
from jax.sharding import PartitionSpec as P

LEARN_BASE = 0.25
MOMENTUM = 0.9


def solution(mesh):
    n_pod = mesh.shape['pod']
    n_data = mesh.shape['data']
    rows_spec = P(('pod', 'data'), None)
    full_spec = P()

    def reduce_grad(grad_low, scatter_dim):
        shard_sum = lax.psum_scatter(grad_low, 'data', scatter_dimension=scatter_dim, tiled=True)
        shard_sum = lax.psum(shard_sum, 'pod')
        return lax.all_gather(shard_sum, 'data', axis=scatter_dim, tiled=True).astype(jnp.float32)

    def train_step(w_first, w_second, m_first, m_second, x_now, y_now, x_next, y_next):
        layers = w_first.shape[0]
        model_width = w_first.shape[1]
        batch_total = x_now.shape[0] * n_pod * n_data
        learn_rate = LEARN_BASE / layers
        wf_low = w_first.astype(jnp.bfloat16)
        ws_low = w_second.astype(jnp.bfloat16)
        hidden = x_now.astype(jnp.float32)
        saved_acts = []
        for layer_idx in range(layers):
            h_low = hidden.astype(jnp.bfloat16)
            pre_act = jnp.dot(h_low, wf_low[layer_idx], preferred_element_type=jnp.float32)
            act_val, gelu_back = jax.vjp(jax.nn.gelu, pre_act)
            act_low = act_val.astype(jnp.bfloat16)
            hidden = hidden + jnp.dot(act_low, ws_low[layer_idx], preferred_element_type=jnp.float32)
            saved_acts.append((h_low, act_low, gelu_back))
        grad_h = (hidden - y_now.astype(jnp.float32)) / (batch_total * model_width)
        sum_first = [None] * layers
        sum_second = [None] * layers
        for layer_idx in reversed(range(layers)):
            h_low, act_low, gelu_back = saved_acts[layer_idx]
            grad_low = grad_h.astype(jnp.bfloat16)
            g_second = jnp.einsum('bf,bd->fd', act_low, grad_low, preferred_element_type=jnp.float32)
            grad_act = jnp.einsum('bd,fd->bf', grad_low, ws_low[layer_idx], preferred_element_type=jnp.float32)
            grad_pre = gelu_back(grad_act)[0].astype(jnp.bfloat16)
            g_first = jnp.einsum('bd,bf->df', h_low, grad_pre, preferred_element_type=jnp.float32)
            if layer_idx > 0:
                grad_h = grad_h + jnp.einsum('bf,df->bd', grad_pre, wf_low[layer_idx], preferred_element_type=jnp.float32)
            sum_second[layer_idx] = reduce_grad(g_second.astype(jnp.bfloat16), 0)
            sum_first[layer_idx] = reduce_grad(g_first.astype(jnp.bfloat16), 1)
        new_wf, new_ws, new_mf, new_ms = [], [], [], []
        hidden = x_next.astype(jnp.float32)
        for layer_idx in range(layers):
            mom_first = MOMENTUM * m_first[layer_idx] + sum_first[layer_idx]
            mom_second = MOMENTUM * m_second[layer_idx] + sum_second[layer_idx]
            weight_first = w_first[layer_idx] - learn_rate * mom_first
            weight_second = w_second[layer_idx] - learn_rate * mom_second
            new_mf.append(mom_first)
            new_ms.append(mom_second)
            new_wf.append(weight_first)
            new_ws.append(weight_second)
            pre_act = jnp.dot(hidden.astype(jnp.bfloat16), weight_first.astype(jnp.bfloat16), preferred_element_type=jnp.float32)
            act_low = jax.nn.gelu(pre_act).astype(jnp.bfloat16)
            hidden = hidden + jnp.dot(act_low, weight_second.astype(jnp.bfloat16), preferred_element_type=jnp.float32)
        resid_rows = hidden - y_next.astype(jnp.float32)
        loss_rows = jnp.sum(resid_rows * resid_rows, axis=-1) / (2 * model_width)
        return (jnp.stack(new_wf), jnp.stack(new_ws), jnp.stack(new_mf), jnp.stack(new_ms), loss_rows, hidden)

    return jax.shard_map(train_step, mesh=mesh,
                         in_specs=(full_spec,) * 4 + (rows_spec,) * 4,
                         out_specs=(full_spec,) * 4 + (P(('pod', 'data')), rows_spec),
                         check_vma=False)
```

profile of v0, /device:TPU:0, one launch (start us, length us, event | category | flops | bytes accessed | tf_op | source)
XLA Modules:
  0.0 1315.3 jit_solution(11156022611568024504)
XLA Ops:
  292.9 20.2 %reduce-scatter.85.cloned.1.call-done = bf16[256,256]{1,0:T(8,128)(2,1)} async-done(((bf16[1024,256]{1,0:T(8,128)(2,1)}), bf16[256,256]{1,0:T(8,128)(2,1)}) %reduce-scatter.85.cloned.1.call-update) | async-done | bytes 131088 | tf_op jit(solution)/shard_map/reduce_scatter | solution.py:17
  313.1 20.3 %reduce-scatter.51.cloned.1.call-done = bf16[256,256]{0,1:T(8,128)(2,1)} async-done(((bf16[256,1024]{0,1:T(8,128)(2,1)}), bf16[256,256]{0,1:T(8,128)(2,1)}) %reduce-scatter.51.cloned.1.call-update) | async-done | bytes 131088 | tf_op jit(solution)/shard_map/reduce_scatter | solution.py:17
  333.4 20.2 %reduce-scatter.83.cloned.1.call-done = bf16[256,256]{1,0:T(8,128)(2,1)} async-done(((bf16[1024,256]{1,0:T(8,128)(2,1)}), bf16[256,256]{1,0:T(8,128)(2,1)}) %reduce-scatter.83.cloned.1.call-update) | async-done | bytes 131088 | tf_op jit(solution)/shard_map/reduce_scatter | solution.py:17
  353.5 20.2 %reduce-scatter.49.cloned.1.call-done = bf16[256,256]{0,1:T(8,128)(2,1)} async-done(((bf16[256,1024]{0,1:T(8,128)(2,1)}), bf16[256,256]{0,1:T(8,128)(2,1)}) %reduce-scatter.49.cloned.1.call-update) | async-done | bytes 131088 | tf_op jit(solution)/shard_map/reduce_scatter | solution.py:17
  373.7 20.2 %reduce-scatter.81.cloned.1.call-done = bf16[256,256]{1,0:T(8,128)(2,1)} async-done(((bf16[1024,256]{1,0:T(8,128)(2,1)}), bf16[256,256]{1,0:T(8,128)(2,1)}) %reduce-scatter.81.cloned.1.call-update) | async-done | bytes 131088 | tf_op jit(solution)/shard_map/reduce_scatter | solution.py:17
  393.9 20.2 %reduce-scatter.47.cloned.1.call-done = bf16[256,256]{0,1:T(8,128)(2,1)} async-done(((bf16[256,1024]{0,1:T(8,128)(2,1)}), bf16[256,256]{0,1:T(8,128)(2,1)}) %reduce-scatter.47.cloned.1.call-update) | async-done | bytes 131088 | tf_op jit(solution)/shard_map/reduce_scatter | solution.py:17
  414.0 20.2 %reduce-scatter.79.cloned.1.call-done = bf16[256,256]{1,0:T(8,128)(2,1)} async-done(((bf16[1024,256]{1,0:T(8,128)(2,1)}), bf16[256,256]{1,0:T(8,128)(2,1)}) %reduce-scatter.79.cloned.1.call-update) | async-done | bytes 131088 | tf_op jit(solution)/shard_map/reduce_scatter | solution.py:17
  434.2 20.3 %reduce-scatter.45.cloned.1.call-done = bf16[256,256]{0,1:T(8,128)(2,1)} async-done(((bf16[256,1024]{0,1:T(8,128)(2,1)}), bf16[256,256]{0,1:T(8,128)(2,1)}) %reduce-scatter.45.cloned.1.call-update) | async-done | bytes 131088 | tf_op jit(solution)/shard_map/reduce_scatter | solution.py:17
  454.5 20.2 %reduce-scatter.77.cloned.1.call-done = bf16[256,256]{1,0:T(8,128)(2,1)} async-done(((bf16[1024,256]{1,0:T(8,128)(2,1)}), bf16[256,256]{1,0:T(8,128)(2,1)}) %reduce-scatter.77.cloned.1.call-update) | async-done | bytes 131088 | tf_op jit(solution)/shard_map/reduce_scatter | solution.py:17
  474.7 20.3 %reduce-scatter.43.cloned.1.call-done = bf16[256,256]{0,1:T(8,128)(2,1)} async-done(((bf16[256,1024]{0,1:T(8,128)(2,1)}), bf16[256,256]{0,1:T(8,128)(2,1)}) %reduce-scatter.43.cloned.1.call-update) | async-done | bytes 131088 | tf_op jit(solution)/shard_map/reduce_scatter | solution.py:17
  495.0 20.3 %reduce-scatter.75.cloned.1.call-done = bf16[256,256]{1,0:T(8,128)(2,1)} async-done(((bf16[1024,256]{1,0:T(8,128)(2,1)}), bf16[256,256]{1,0:T(8,128)(2,1)}) %reduce-scatter.75.cloned.1.call-update) | async-done | bytes 131088 | tf_op jit(solution)/shard_map/reduce_scatter | solution.py:17
  515.3 20.3 %reduce-scatter.41.cloned.1.call-done = bf16[256,256]{0,1:T(8,128)(2,1)} async-done(((bf16[256,1024]{0,1:T(8,128)(2,1)}), bf16[256,256]{0,1:T(8,128)(2,1)}) %reduce-scatter.41.cloned.1.call-update) | async-done | bytes 131088 | tf_op jit(solution)/shard_map/reduce_scatter | solution.py:17
  535.6 20.2 %reduce-scatter.73.cloned.1.call-done = bf16[256,256]{1,0:T(8,128)(2,1)} async-done(((bf16[1024,256]{1,0:T(8,128)(2,1)}), bf16[256,256]{1,0:T(8,128)(2,1)}) %reduce-scatter.73.cloned.1.call-update) | async-done | bytes 131088 | tf_op jit(solution)/shard_map/reduce_scatter | solution.py:17
  555.8 20.3 %reduce-scatter.39.cloned.1.call-done = bf16[256,256]{0,1:T(8,128)(2,1)} async-done(((bf16[256,1024]{0,1:T(8,128)(2,1)}), bf16[256,256]{0,1:T(8,128)(2,1)}) %reduce-scatter.39.cloned.1.call-update) | async-done | bytes 131088 | tf_op jit(solution)/shard_map/reduce_scatter | solution.py:17
  576.1 20.2 %reduce-scatter.71.cloned.1.call-done = bf16[256,256]{1,0:T(8,128)(2,1)} async-done(((bf16[1024,256]{1,0:T(8,128)(2,1)}), bf16[256,256]{1,0:T(8,128)(2,1)}) %reduce-scatter.71.cloned.1.call-update) | async-done | bytes 131088 | tf_op jit(solution)/shard_map/reduce_scatter | solution.py:17
  596.3 20.2 %reduce-scatter.37.cloned.1.call-done = bf16[256,256]{0,1:T(8,128)(2,1)} async-done(((bf16[256,1024]{0,1:T(8,128)(2,1)}), bf16[256,256]{0,1:T(8,128)(2,1)}) %reduce-scatter.37.cloned.1.call-update) | async-done | bytes 131088 | tf_op jit(solution)/shard_map/reduce_scatter | solution.py:17
  616.5 20.3 %reduce-scatter.69.cloned.1.call-done = bf16[256,256]{1,0:T(8,128)(2,1)} async-done(((bf16[1024,256]{1,0:T(8,128)(2,1)}), bf16[256,256]{1,0:T(8,128)(2,1)}) %reduce-scatter.69.cloned.1.call-update) | async-done | bytes 131088 | tf_op jit(solution)/shard_map/reduce_scatter | solution.py:17
  636.8 20.9 %reduce-scatter.35.cloned.1.call-done = bf16[256,256]{0,1:T(8,128)(2,1)} async-done(((bf16[256,1024]{0,1:T(8,128)(2,1)}), bf16[256,256]{0,1:T(8,128)(2,1)}) %reduce-scatter.35.cloned.1.call-update) | async-done | bytes 131088 | tf_op jit(solution)/shard_map/reduce_scatter | solution.py:17
  657.7 20.2 %reduce-scatter.65.cloned.1.call-done = bf16[256,256]{1,0:T(8,128)(2,1)} async-done(((bf16[1024,256]{1,0:T(8,128)(2,1)}), bf16[256,256]{1,0:T(8,128)(2,1)}) %reduce-scatter.65.cloned.1.call-update) | async-done | bytes 131088 | tf_op jit(solution)/shard_map/reduce_scatter | solution.py:17
  677.8 20.9 %reduce-scatter.33.cloned.1.call-done = bf16[256,256]{0,1:T(8,128)(2,1)} async-done(((bf16[256,1024]{0,1:T(8,128)(2,1)}), bf16[256,256]{0,1:T(8,128)(2,1)}) %reduce-scatter.33.cloned.1.call-update) | async-done | bytes 131088 | tf_op jit(solution)/shard_map/reduce_scatter | solution.py:17
  698.7 20.9 %reduce-scatter.67.cloned.1.call-done = bf16[256,256]{1,0:T(8,128)(2,1)} async-done(((bf16[1024,256]{1,0:T(8,128)(2,1)}), bf16[256,256]{1,0:T(8,128)(2,1)}) %reduce-scatter.67.cloned.1.call-update) | async-done | bytes 131088 | tf_op jit(solution)/shard_map/reduce_scatter | solution.py:17
  721.7 11.4 fusion.567
  770.2 11.0 fusion.566
  816.4 43.7 %all-reduce.3.cloned.1.call-done = (bf16[256,256]{0,1:T(8,128)(2,1)}, bf16[256,256]{0,1:T(8,128)(2,1)}, bf16[256,256]{0,1:T(8,128)(2,1)}, bf16[256,256]{0,1:T(8,...) async-done(((bf16[256,256]{0,1:T(8,128)(2,1)}, ...) | async-done | bytes 4194320 | tf_op jit(solution)/shard_map/psum | solution.py:18
  867.5 8.1 all_gather.97
  875.5 8.4 all_gather.98
  883.9 8.0 all_gather.99
  891.9 8.4 all_gather.100
  900.3 8.0 all_gather.101
  908.2 8.6 all_gather.102
  1228.2 17.6 %copy.65 = f32[16,256,1024]{2,1,0:T(8,128)} copy(f32[16,256,1024]{1,2,0:T(8,128)} %get-tuple-element.108) | data formatting | bytes 33554432
  1245.8 17.7 %copy.64 = f32[16,256,1024]{2,1,0:T(8,128)} copy(f32[16,256,1024]{1,2,0:T(8,128)} %get-tuple-element.109) | data formatting | bytes 33554432
  (688 shorter events, 721.0 us)
Async XLA Ops:
  7.2 278.4 %reduce-scatter.63.cloned.1.call-start = ((), (), s32[]{:S(2)}) async-start(), calls=%async_computation.47 | async-start | bytes 655360 | tf_op jit(solution)/shard_map/reduce_scatter | solution.py:17
  69.5 216.1 %reduce-scatter.95.cloned.1.call-start = ((), (), s32[]{:S(2)}) async-start(), calls=%async_computation.63 | async-start | bytes 655360 | tf_op jit(solution)/shard_map/reduce_scatter | solution.py:17
  74.4 211.2 %reduce-scatter.61.cloned.1.call-start = ((), (), s32[]{:S(2)}) async-start(), calls=%async_computation.46 | async-start | bytes 655360 | tf_op jit(solution)/shard_map/reduce_scatter | solution.py:17
  83.3 202.4 %reduce-scatter.93.cloned.1.call-start = ((), (), s32[]{:S(2)}) async-start(), calls=%async_computation.62 | async-start | bytes 655360 | tf_op jit(solution)/shard_map/reduce_scatter | solution.py:17
  88.1 197.6 %reduce-scatter.59.cloned.1.call-start = ((), (), s32[]{:S(2)}) async-start(), calls=%async_computation.45 | async-start | bytes 655360 | tf_op jit(solution)/shard_map/reduce_scatter | solution.py:17
  97.2 188.5 %reduce-scatter.91.cloned.1.call-start = ((), (), s32[]{:S(2)}) async-start(), calls=%async_computation.61 | async-start | bytes 655360 | tf_op jit(solution)/shard_map/reduce_scatter | solution.py:17
  102.5 183.2 %reduce-scatter.57.cloned.1.call-start = ((), (), s32[]{:S(2)}) async-start(), calls=%async_computation.44 | async-start | bytes 655360 | tf_op jit(solution)/shard_map/reduce_scatter | solution.py:17
  111.4 174.3 %reduce-scatter.89.cloned.1.call-start = ((), (), s32[]{:S(2)}) async-start(), calls=%async_computation.60 | async-start | bytes 655360 | tf_op jit(solution)/shard_map/reduce_scatter | solution.py:17
  116.7 169.1 %reduce-scatter.55.cloned.1.call-start = ((), (), s32[]{:S(2)}) async-start(), calls=%async_computation.43 | async-start | bytes 655360 | tf_op jit(solution)/shard_map/reduce_scatter | solution.py:17
  131.1 161.8 %reduce-scatter.53.cloned.1.call-start = ((), (), s32[]{:S(2)}) async-start(), calls=%async_computation.42 | async-start | bytes 655360 | tf_op jit(solution)/shard_map/reduce_scatter | solution.py:17
  140.0 173.1 %reduce-scatter.85.cloned.1.call-start = ((), (), s32[]{:S(2)}) async-start(), calls=%async_computation.58 | async-start | bytes 655360 | tf_op jit(solution)/shard_map/reduce_scatter | solution.py:17
  145.3 188.1 %reduce-scatter.51.cloned.1.call-start = ((), (), s32[]{:S(2)}) async-start(), calls=%async_computation.41 | async-start | bytes 655360 | tf_op jit(solution)/shard_map/reduce_scatter | solution.py:17
  154.4 199.1 %reduce-scatter.83.cloned.1.call-start = ((), (), s32[]{:S(2)}) async-start(), calls=%async_computation.57 | async-start | bytes 655360 | tf_op jit(solution)/shard_map/reduce_scatter | solution.py:17
  159.7 214.1 %reduce-scatter.49.cloned.1.call-start = ((), (), s32[]{:S(2)}) async-start(), calls=%async_computation.40 | async-start | bytes 655360 | tf_op jit(solution)/shard_map/reduce_scatter | solution.py:17
  168.5 225.3 %reduce-scatter.81.cloned.1.call-start = ((), (), s32[]{:S(2)}) async-start(), calls=%async_computation.56 | async-start | bytes 655360 | tf_op jit(solution)/shard_map/reduce_scatter | solution.py:17
  173.8 240.3 %reduce-scatter.47.cloned.1.call-start = ((), (), s32[]{:S(2)}) async-start(), calls=%async_computation.39 | async-start | bytes 655360 | tf_op jit(solution)/shard_map/reduce_scatter | solution.py:17
  182.9 251.3 %reduce-scatter.79.cloned.1.call-start = ((), (), s32[]{:S(2)}) async-start(), calls=%async_computation.55 | async-start | bytes 655360 | tf_op jit(solution)/shard_map/reduce_scatter | solution.py:17
  188.1 266.4 %reduce-scatter.45.cloned.1.call-start = ((), (), s32[]{:S(2)}) async-start(), calls=%async_computation.38 | async-start | bytes 655360 | tf_op jit(solution)/shard_map/reduce_scatter | solution.py:17
  197.0 277.6 %reduce-scatter.77.cloned.1.call-start = ((), (), s32[]{:S(2)}) async-start(), calls=%async_computation.54 | async-start | bytes 655360 | tf_op jit(solution)/shard_map/reduce_scatter | solution.py:17
  202.3 292.7 %reduce-scatter.43.cloned.1.call-start = ((), (), s32[]{:S(2)}) async-start(), calls=%async_computation.37 | async-start | bytes 655360 | tf_op jit(solution)/shard_map/reduce_scatter | solution.py:17
  211.5 303.9 %reduce-scatter.75.cloned.1.call-start = ((), (), s32[]{:S(2)}) async-start(), calls=%async_computation.53 | async-start | bytes 655360 | tf_op jit(solution)/shard_map/reduce_scatter | solution.py:17
  216.7 318.9 %reduce-scatter.41.cloned.1.call-start = ((), (), s32[]{:S(2)}) async-start(), calls=%async_computation.36 | async-start | bytes 655360 | tf_op jit(solution)/shard_map/reduce_scatter | solution.py:17
  225.6 330.2 %reduce-scatter.73.cloned.1.call-start = ((), (), s32[]{:S(2)}) async-start(), calls=%async_computation.52 | async-start | bytes 655360 | tf_op jit(solution)/shard_map/reduce_scatter | solution.py:17
  230.9 345.2 %reduce-scatter.39.cloned.1.call-start = ((), (), s32[]{:S(2)}) async-start(), calls=%async_computation.35 | async-start | bytes 655360 | tf_op jit(solution)/shard_map/reduce_scatter | solution.py:17
  240.1 356.2 %reduce-scatter.71.cloned.1.call-start = ((), (), s32[]{:S(2)}) async-start(), calls=%async_computation.51 | async-start | bytes 655360 | tf_op jit(solution)/shard_map/reduce_scatter | solution.py:17
  245.3 371.1 %reduce-scatter.37.cloned.1.call-start = ((), (), s32[]{:S(2)}) async-start(), calls=%async_computation.34 | async-start | bytes 655360 | tf_op jit(solution)/shard_map/reduce_scatter | solution.py:17
  254.2 382.6 %reduce-scatter.69.cloned.1.call-start = ((), (), s32[]{:S(2)}) async-start(), calls=%async_computation.50 | async-start | bytes 655360 | tf_op jit(solution)/shard_map/reduce_scatter | solution.py:17
  259.5 398.2 %reduce-scatter.35.cloned.1.call-start = ((), (), s32[]{:S(2)}) async-start(), calls=%async_computation.33 | async-start | bytes 655360 | tf_op jit(solution)/shard_map/reduce_scatter | solution.py:17
  268.6 409.3 %reduce-scatter.65.cloned.1.call-start = ((), (), s32[]{:S(2)}) async-start(), calls=%async_computation.48 | async-start | bytes 655360 | tf_op jit(solution)/shard_map/reduce_scatter | solution.py:17
  274.0 424.8 %reduce-scatter.33.cloned.1.call-start = ((), (), s32[]{:S(2)}) async-start(), calls=%async_computation.32 | async-start | bytes 655360 | tf_op jit(solution)/shard_map/reduce_scatter | solution.py:17
  280.6 439.0 %reduce-scatter.67.cloned.1.call-start = ((), (), s32[]{:S(2)}) async-start(), calls=%async_computation.49 | async-start | bytes 655360 | tf_op jit(solution)/shard_map/reduce_scatter | solution.py:17
  285.5 574.7 %all-reduce.3.cloned.1.call-start = ((), (), s32[]{:S(2)}) async-start(), calls=%async_computation.64 | async-start | bytes 8388608 | tf_op jit(solution)/shard_map/psum | solution.py:18
  (203 other events, 5098.3 us)
Sparse Core Ops, SparseCore 0:
  69.6 20.6 reduce-scatter.62
  92.8 17.7 reduce-scatter.94
  113.1 17.7 reduce-scatter.60
  133.3 17.7 reduce-scatter.92
  153.4 17.7 reduce-scatter.58
  173.6 17.7 reduce-scatter.90
  193.9 17.7 reduce-scatter.56
  214.2 17.7 reduce-scatter.88
  234.6 17.7 reduce-scatter.54
  254.7 17.7 reduce-scatter.86
  275.0 17.7 reduce-scatter.52
  295.2 17.7 reduce-scatter.84
  315.5 17.7 reduce-scatter.50
  335.7 17.7 reduce-scatter.82
  355.9 17.7 reduce-scatter.48
  396.2 17.7 reduce-scatter.46
  416.4 17.7 reduce-scatter.78
  436.7 17.7 reduce-scatter.44
  456.8 17.7 reduce-scatter.76
  477.2 17.7 reduce-scatter.42
  497.5 17.7 reduce-scatter.74
  517.8 17.7 reduce-scatter.40
  538.0 17.7 reduce-scatter.72
  558.3 17.7 reduce-scatter.38
  578.5 17.7 reduce-scatter.70
  598.6 17.7 reduce-scatter.36
  618.9 17.7 reduce-scatter.68
  639.8 17.7 reduce-scatter.34
  660.0 17.7 reduce-scatter.64
  680.9 17.7 reduce-scatter.32
  701.8 17.7 reduce-scatter.66
  725.9 134.2 all-reduce.2
  (1 shorter events, 17.7 us)
where the time goes:
time: 1330 us; the launch traced here: 1320 us
  waiting for transfers between devices  478 us (36%)
  matrix products  344 us (26%)
  blocking collectives  239 us (18%)
  local copies, waits for them, and re-layouts  154 us (12%)
  other arithmetic  82.7 us (6%)
  between operations  16.8 us (1%)
    reduce_scatter x32, waiting for transfers between devices, reduce_grad(): lax.psum_scatter(grad_low, 'data', scatter_dimension=scatter_dim, tiled=T...  434 us
    all_gather x32, blocking collectives, reduce_grad(): lax.all_gather(shard_sum, 'data', axis=scatter_dim, tiled=True)  239 us
    unnamed x441, local copies, waits for them, and re-layouts  131 us
    dot_general x16, matrix products, train_step(): jnp.dot(act_low, weight_second.astype(jnp.bfloat16), preferred_element_ty...  95.7 us
    dot_general x16, matrix products, train_step(): jnp.einsum('bf,bd->fd', act_low, grad_low, preferred_element_type=jnp.flo...  79.2 us
    dot_general x15, matrix products, train_step(): jnp.einsum('bd,fd->bf', grad_low, ws_low[layer_idx], preferred_element_ty...  70.2 us
    unnamed x31, other arithmetic  70 us
    psum x1, waiting for transfers between devices, reduce_grad(): shard_sum = lax.psum(shard_sum, 'pod')  43.7 us
  transfers between devices with their start and end apart: 33, of which 23 were waited for; matrix products, arithmetic and copies ran while one was open for 23% of the time, Pallas kernels for 0%

commit v1 on v0

v1 whole, which is shorter than its diff:
```python
import functools

import jax
import jax.numpy as jnp
from jax import lax
from jax.experimental import pallas as pl
from jax.experimental.pallas import tpu as pltpu
from jax.sharding import PartitionSpec as P

LEARN_BASE = 0.25
MOMENTUM = 0.9
C0 = 0.7978845608028654
C1 = C0 * 0.044715
MESH = pl.DeviceIdType.MESH
F32 = jnp.float32
BF16 = jnp.bfloat16
VMEM_LIMIT = 67_000_000

ORDERS = (("x", "y", "z"), ("y", "z", "x"), ("z", "x", "y"))
RING = 6
LAGS = (0, 1, 3, 4, 5, 6, 7, 9, 10)


def dot(a, b, ca=1, cb=0):
    return lax.dot_general(a, b, (((ca,), (cb,)), ((), ())), preferred_element_type=F32)


def gelu(a):
    t = jnp.tanh(a * (C0 + C1 * (a * a)))
    half = 0.5 * a
    return half + half * t


def gelu_both(a):
    a2 = a * a
    t = jnp.tanh(a * (C0 + C1 * a2))
    s = 0.5 + 0.5 * t
    u = a * s
    return u, s + u * (1.0 - s) * (2.0 * C0 + (6.0 * C1) * a2)


def layer_forward(h_ref, w1b_ref, w2b_ref, u_ref, hs_ref, chunk, tile):
    rows, width = h_ref.shape[0], w1b_ref.shape[1]
    for r in range(0, rows, chunk):
        hb = h_ref[r:r + chunk, :].astype(BF16)
        if hs_ref is not None:
            hs_ref[r:r + chunk, :] = hb
        for n in range(0, width, tile):
            u_ref[r:r + chunk, n:n + tile] = gelu(dot(hb, w1b_ref[:, n:n + tile])).astype(BF16)
        h_ref[r:r + chunk, :] = h_ref[r:r + chunk, :] + dot(u_ref[r:r + chunk, :], w2b_ref[...])


def forward_kernel(scale, x_ref, y_ref, w1_ref, w2_ref, hs_ref, w1b_ref, w2b_ref, g_ref, h_ref, u_ref):
    layer = pl.program_id(0)

    @pl.when(layer == 0)
    def _():
        h_ref[...] = x_ref[...].astype(F32)

    w1b_ref[...] = w1_ref[...].astype(BF16)
    w2b_ref[...] = w2_ref[...].astype(BF16)
    layer_forward(h_ref, w1b_ref, w2b_ref, u_ref, hs_ref, 256, 256)

    @pl.when(layer == pl.num_programs(0) - 1)
    def _():
        g_ref[...] = (h_ref[...] - y_ref[...].astype(F32)) * scale


def update_kernel(rate, x_ref, y_ref, w1_ref, w2_ref, m1_ref, m2_ref, gr_ref,
                  w1o_ref, w2o_ref, m1o_ref, m2o_ref, loss_ref, h_ref, w1b_ref, w2b_ref, u_ref):
    layer = pl.program_id(0)
    width = w1_ref.shape[0]

    @pl.when(layer == 0)
    def _():
        h_ref[...] = x_ref[...].astype(F32)

    mom = MOMENTUM * m1_ref[...] + gr_ref[:width, :].astype(F32)
    m1o_ref[...] = mom
    new = w1_ref[...] - rate * mom
    w1o_ref[...] = new
    w1b_ref[...] = new.astype(BF16)
    mom = MOMENTUM * m2_ref[...] + gr_ref[width:, :].astype(F32).T
    m2o_ref[...] = mom
    new = w2_ref[...] - rate * mom
    w2o_ref[...] = new
    w2b_ref[...] = new.astype(BF16)
    layer_forward(h_ref, w1b_ref, w2b_ref, u_ref, None, 256, 256)

    @pl.when(layer == pl.num_programs(0) - 1)
    def _():
        resid = h_ref[...] - y_ref[...].astype(F32)
        loss_ref[...] = jnp.sum((resid * resid).T, axis=0, keepdims=True) / (2 * width)


def backward_kernel(layers, g0_ref, w1_ref, w2_ref, hs_ref, out_ref,
                    g_ref, gb_ref, gt_ref, ht_ref, u_ref, q_ref,
                    grad_ref, sum_ref, r0_ref, r1_ref, r2_ref, r3_ref, send_sem, recv_sem, out_sem):
    it = pl.program_id(0)
    pod, data = lax.axis_index("pod"), lax.axis_index("data")
    z, y, x, c = pod // 2, pod % 2, data // 2, data % 2
    bits = {"x": x, "y": y, "z": z}
    peers = {
        "core": (pod, x * 2 + (1 - c)),
        "x": (pod, (1 - x) * 2 + c),
        "y": (z * 2 + (1 - y), data),
        "z": ((1 - z) * 2 + y, data),
    }
    rows, width = g_ref.shape
    hidden = u_ref.shape[1]
    block = 2 * width
    recv_refs = (r0_ref, r1_ref, r2_ref, r3_ref)
    third = hidden // 128 * 3 // 8 * 128
    parts = ((0, third), (third, third), (2 * third, hidden - 2 * third))

    @pl.when(it == 0)
    def _():
        barrier = pltpu.get_barrier_semaphore()
        for peer in peers.values():
            pl.semaphore_signal(barrier, inc=1, device_id=peer, device_id_type=MESH)
        pl.semaphore_wait(barrier, 4)
        g_ref[...] = g0_ref[...]

    def ring(slot):
        return slot % RING

    def region(part, k):
        offset = c * (block // 2)
        for n in range(k - 1):
            offset = offset + bits[ORDERS[part][n]] * (block >> (n + 2))
        return offset

    def message(slot, m, part):
        if m in (0, 7):
            size = block // 2
            mine, other = c * size, (1 - c) * size
            cols = slice(None)
            axis = "core"
            stage = 0
        else:
            stage = m if m <= 3 else 7 - m
            axis = ORDERS[part][stage - 1]
            size = block >> (stage + 1)
            base = region(part, stage)
            mine, other = base + bits[axis] * size, base + (1 - bits[axis]) * size
            cols = pl.ds(parts[part][0], parts[part][1])
        if m <= 3:
            src = grad_ref.at[ring(slot), pl.ds(pl.multiple_of(other, 16), size), cols]
            dst = recv_refs[stage].at[slot, :, cols]
        else:
            src = sum_ref.at[slot, pl.ds(pl.multiple_of(mine, 16), size), cols]
            dst = src
        return pltpu.make_async_remote_copy(
            src_ref=src, dst_ref=dst, send_sem=send_sem.at[slot, m, part], recv_sem=recv_sem.at[slot, m, part],
            device_id=peers[axis], device_id_type=MESH)

    def parts_of(m):
        return (0,) if m in (0, 7) else (0, 1, 2)

    def accumulate(slot, stage, part):
        size = block >> (stage + 1)
        if stage == 0:
            mine, cols = c * size, pl.ds(0, hidden)
        else:
            mine, cols = region(part, stage + 1), pl.ds(*parts[part])
        where = pl.ds(pl.multiple_of(mine, 16), size)
        total = grad_ref[ring(slot), where, cols].astype(F32) + recv_refs[stage][slot, :, cols].astype(F32)
        if stage == 3:
            sum_ref[slot, where, cols] = total.astype(BF16)
        else:
            grad_ref[ring(slot), where, cols] = total.astype(BF16)

    def result_copy(slot):
        return pltpu.make_async_copy(sum_ref.at[slot], out_ref.at[slot], out_sem.at[slot])

    def step(s, slot):
        if s > 0:
            m = s - 1
            for part in parts_of(m):
                message(slot, m, part).wait()
                if m <= 3:
                    accumulate(slot, m, part)
                if m not in (0, 7) and s < 8 and s != 7:
                    message(slot, s, part).start()
        if s == 0 or s == 1 or s == 7:
            for part in parts_of(s):
                message(slot, s, part).start()
        if s == 8:
            result_copy(slot).start()

    def comm_point(parity):
        for s in reversed(range(9)):
            if LAGS[s] % 2 == parity:
                done = it - 1 - (LAGS[s] - parity) // 2

                @pl.when(done >= 0)
                def _():
                    step(s, layers - 1 - done)

    tile, chunk = 256, 256
    comm_point(0)

    gb_ref[...] = g_ref[...].astype(BF16)
    gt_ref[...] = gb_ref[...].T
    ht_ref[...] = hs_ref[...].T

    def half(tiles):
        for n in tiles:
            cols = slice(n, n + tile)
            for r in range(0, rows, chunk):
                a = dot(hs_ref[r:r + chunk, :], w1_ref[:, cols])
                gu = dot(gb_ref[r:r + chunk, :], w2_ref[cols, :], 1, 1)
                u, slope = gelu_both(a)
                u_ref[r:r + chunk, cols] = u.astype(BF16)
                q_ref[r:r + chunk, cols] = (slope * gu).astype(BF16)
            layer = layers - 1 - it
            grad_ref[ring(layer), width:, cols] = dot(gt_ref[...], u_ref[:, cols]).astype(BF16)
            grad_ref[ring(layer), :width, cols] = dot(ht_ref[...], q_ref[:, cols]).astype(BF16)
            for r in range(0, rows, chunk):
                g_ref[r:r + chunk, :] = g_ref[r:r + chunk, :] + dot(q_ref[r:r + chunk, cols], w1_ref[:, cols], 1, 1)

    tiles = list(range(0, hidden, tile))
    half(tiles[:len(tiles) // 2])
    comm_point(1)
    half(tiles[len(tiles) // 2:])

    @pl.when(it == layers - 1)
    def _():
        for tick in range(2 * layers, 2 * layers + LAGS[8] + 1):
            for s in reversed(range(9)):
                if (tick - LAGS[s]) % 2 == 0:
                    done = (tick - 2 - LAGS[s]) // 2
                    if 0 <= done < layers:
                        step(s, layers - 1 - done)
        for slot in range(layers):
            result_copy(slot).wait()


def solution(mesh):
    n_pod = mesh.shape['pod']
    n_data = mesh.shape['data']
    rows_spec = P(('pod', 'data'), None)
    full_spec = P()

    def train_step(w_first, w_second, m_first, m_second, x_now, y_now, x_next, y_next):
        layers, width, hidden = w_first.shape
        rows = x_now.shape[0]
        batch = rows * n_pod * n_data
        whole = lambda *shape: pl.BlockSpec(shape, lambda i: (0,) * len(shape))
        per_layer = lambda *shape: pl.BlockSpec((None,) + shape, lambda i: (i, 0, 0))
        reverse = lambda *shape: pl.BlockSpec((None,) + shape, lambda i: (layers - 1 - i, 0, 0))
        shape = jax.ShapeDtypeStruct
        matmul_flops = 2 * rows * width * hidden * layers

        hs, w1b, w2b, g0 = pl.pallas_call(
            functools.partial(forward_kernel, 1.0 / (batch * width)),
            grid=(layers,),
            in_specs=[whole(rows, width), whole(rows, width), per_layer(width, hidden), per_layer(hidden, width)],
            out_specs=[per_layer(rows, width), per_layer(width, hidden), per_layer(hidden, width), whole(rows, width)],
            out_shape=[shape((layers, rows, width), BF16), shape((layers, width, hidden), BF16),
                       shape((layers, hidden, width), BF16), shape((rows, width), F32)],
            scratch_shapes=[pltpu.VMEM((rows, width), F32), pltpu.VMEM((rows, hidden), BF16)],
            compiler_params=pltpu.CompilerParams(dimension_semantics=("arbitrary",), vmem_limit_bytes=VMEM_LIMIT),
            cost_estimate=pl.CostEstimate(flops=2 * matmul_flops, bytes_accessed=60_000_000, transcendentals=0),
            name="forward_now",
        )(x_now, y_now, w_first, w_second)

        grads = pl.pallas_call(
            functools.partial(backward_kernel, layers),
            grid=(layers,),
            in_specs=[whole(rows, width), reverse(width, hidden), reverse(hidden, width), reverse(rows, width)],
            out_specs=pl.BlockSpec(memory_space=pl.ANY),
            out_shape=shape((layers, 2 * width, hidden), BF16),
            scratch_shapes=[
                pltpu.VMEM((rows, width), F32),
                pltpu.VMEM((rows, width), BF16),
                pltpu.VMEM((width, rows), BF16),
                pltpu.VMEM((width, rows), BF16),
                pltpu.VMEM((rows, hidden), BF16),
                pltpu.VMEM((rows, hidden), BF16),
                pltpu.VMEM((RING, 2 * width, hidden), BF16),
                pltpu.VMEM((layers, 2 * width, hidden), BF16),
                pltpu.VMEM((layers, width, hidden), BF16),
                pltpu.VMEM((layers, width // 2, hidden), BF16),
                pltpu.VMEM((layers, width // 4, hidden), BF16),
                pltpu.VMEM((layers, width // 8, hidden), BF16),
                pltpu.SemaphoreType.DMA((layers, 8, 3)),
                pltpu.SemaphoreType.DMA((layers, 8, 3)),
                pltpu.SemaphoreType.DMA((layers,)),
            ],
            compiler_params=pltpu.CompilerParams(dimension_semantics=("arbitrary",), vmem_limit_bytes=VMEM_LIMIT,
                                                 collective_id=0, has_side_effects=True),
            cost_estimate=pl.CostEstimate(flops=5 * matmul_flops, bytes_accessed=60_000_000, transcendentals=0),
            name="backward_reduce",
        )(g0, w1b, w2b, hs)

        outs = pl.pallas_call(
            functools.partial(update_kernel, LEARN_BASE / layers),
            grid=(layers,),
            in_specs=[whole(rows, width), whole(rows, width), per_layer(width, hidden), per_layer(hidden, width),
                      per_layer(width, hidden), per_layer(hidden, width), per_layer(2 * width, hidden)],
            out_specs=[per_layer(width, hidden), per_layer(hidden, width), per_layer(width, hidden),
                       per_layer(hidden, width), whole(1, rows), whole(rows, width)],
            out_shape=[shape((layers, width, hidden), F32), shape((layers, hidden, width), F32),
                       shape((layers, width, hidden), F32), shape((layers, hidden, width), F32),
                       shape((1, rows), F32), shape((rows, width), F32)],
            scratch_shapes=[pltpu.VMEM((width, hidden), BF16), pltpu.VMEM((hidden, width), BF16),
                            pltpu.VMEM((rows, hidden), BF16)],
            compiler_params=pltpu.CompilerParams(dimension_semantics=("arbitrary",), vmem_limit_bytes=VMEM_LIMIT),
            cost_estimate=pl.CostEstimate(flops=2 * matmul_flops, bytes_accessed=160_000_000, transcendentals=0),
            name="update_forward_next",
        )(x_next, y_next, w_first, w_second, m_first, m_second, grads)
        return outs[0], outs[1], outs[2], outs[3], outs[4].reshape(rows), outs[5]

    return jax.shard_map(train_step, mesh=mesh,
                         in_specs=(full_spec,) * 4 + (rows_spec,) * 4,
                         out_specs=(full_spec,) * 4 + (P(('pod', 'data')), rows_spec),
                         check_vma=False)
```

time: 1330 us -> 256 us (0.19); the launches traced: 1320 us -> 255 us
  waiting for transfers between devices: 478 us -> 0 us
  matrix products: 344 us -> 0 us
  Pallas kernels: 0 us -> 255 us
  blocking collectives: 239 us -> 0 us
  local copies, waits for them, and re-layouts: 154 us -> 0 us
  other arithmetic: 82.7 us -> 0 us
  between operations: 16.8 us -> 0.64 us
    reduce_scatter x32 -> x0, waiting for transfers between devices: 434 us -> none  [reduce_grad(): lax.psum_scatter(grad_low, 'data', scatter_dimension=scatter_dim, tiled=T...]
    dot_general x110 -> x0, matrix products: 344 us -> none  [the longest x16 95.7 us: train_step(): jnp.dot(act_low, weight_second.astype(jnp.bfloat16), preferred_element_ty...]
    pallas_call x0 -> x3, Pallas kernels: none -> 255 us  [the longest x1 160 us: train_step(): pl.pallas_call(functools.partial(backward_kernel, layers), grid=(layers,)...]
    all_gather x32 -> x0, blocking collectives: 239 us -> none  [reduce_grad(): lax.all_gather(shard_sum, 'data', axis=scatter_dim, tiled=True)]
    unnamed x441 -> x0, local copies, waits for them, and re-layouts: 131 us -> none
    unnamed x31 -> x0, other arithmetic: 70 us -> none
    psum x1 -> x0, waiting for transfers between devices: 43.7 us -> none  [reduce_grad(): shard_sum = lax.psum(shard_sum, 'pod')]
    slice x2 -> x0, local copies, waits for them, and re-layouts: 22.5 us -> none  [the longest x1 11.4 us: train_step(): mom_first = MOMENTUM * m_first[layer_idx] + sum_first[layer_idx]]
  transfers between devices with their start and end apart: 33 -> 0, of which waited for: 23 -> 0; matrix products, arithmetic and copies ran while one was open for 23% -> 0% of each run, Pallas kernels for 0% -> 0%
where the time goes in v1:
time: 256 us; the launch traced here: 255 us
  Pallas kernels  255 us (100%)
    pallas_call x1, Pallas kernels, train_step(): pl.pallas_call(functools.partial(backward_kernel, layers), grid=(layers,)...  160 us
    pallas_call x1, Pallas kernels, train_step(): pl.pallas_call(functools.partial(update_kernel, LEARN_BASE / layers), gri...  60.8 us
    pallas_call x1, Pallas kernels, train_step(): pl.pallas_call(functools.partial(forward_kernel, 1.0 / (batch * width)),...  33.5 us

profile of v1, /device:TPU:0, one launch (start us, length us, event | category | flops | bytes accessed | tf_op | source)
XLA Modules:
  0.0 255.3 jit_solution(2767090834845894467)
XLA Ops:
  0.6 33.5 %forward_now.1 = (bf16[16,1024,256]{2,1,0:T(8,128)(2,1)}, bf16[16,256,1024]{2,1,0:T(8,128)(2,1)}, bf16[16,1024,256]{2,1,0:T(8,128)(2,1)}, f32[1024,256]{1,0:T(8,128)}) custom-call(bf16[1024,256]{1,0:T(8,128)(2,1)} %x_ref.2, bf16[1024,256]{1,0:T(8,128)(2,1)} %y_ref.2, f32[16,256,1024]{2,1,0:T(8,128)} %w1_ref.3, f32[16,1024,256]{2,1,0:T(8,128)} %w2_ref.3), custom_call_target="tpu_custom_call" | custom-call | flops 17179869184 | bytes 60000000 | tf_op jit(solution)/shard_map/forward_now/pallas_call | solution.py:255
  34.1 160.4 %backward_reduce.1.gr_ref = bf16[16,512,1024]{2,1,0:T(8,128)(2,1)} custom-call(f32[1024,256]{1,0:T(8,128)} %get-tuple-element.16.g0_ref, bf16[16,256,1024]{2,1,0:T(8,128)(2,1)} %get-tuple-element.17.w1_ref, bf16[16,1024,256]{2,1,0:T(8,128)(2,1)} %get-tuple-element.18.w2_ref, bf16[16,1024,256]{2,1,0:T(8,128)(2,1)} %get-tuple-element.19.hs_ref), custom_call_target="tpu_custom_call" | custom-call | flops 42949672960 | bytes 60000000 | tf_op jit(solution)/shard_map/backward_reduce/pallas_call | solution.py:268
  194.5 60.8 %update_forward_next.1 = (f32[16,256,1024]{2,1,0:T(8,128)}, f32[16,1024,256]{2,1,0:T(8,128)}, f32[16,256,1024]{2,1,0:T(8,128)}, f32[16,1024,256]{2,1,0:T(8,128)}...) custom-call(bf16[1024,256]{1,0:T(8,128)(2,1)} %x_ref.3, bf16[1024,256]{1,0:T(8,128)(2,1)} %y_ref.3, f32[16,256,1024]{2,1,0:T(8,128)} %w1_ref.3, ...), custom_call_target="tpu_custom_call" | custom-call | flops 17179869184 | bytes 160000000 | tf_op jit(solution)/shard_map/update_forward_next/pallas_call | solution.py:297

commit v2 on v1

--- a/solution.py
+++ b/solution.py
@@ -11,32 +11,33 @@
 MOMENTUM = 0.9
 C0 = 0.7978845608028654
 C1 = C0 * 0.044715
+H0, H1 = 2.0 * C0, 8.0 * C1
 MESH = pl.DeviceIdType.MESH
 F32 = jnp.float32
 BF16 = jnp.bfloat16
 VMEM_LIMIT = 67_000_000
 
-ORDERS = (("x", "y", "z"), ("y", "z", "x"), ("z", "x", "y"))
+LAGS = (0, 2, 4, 6, 7, 9, 11, 13, 15)
 RING = 6
-LAGS = (0, 1, 3, 4, 5, 6, 7, 9, 10)
+SLOTS = 6
+AHEAD = 4
 
 
 def dot(a, b, ca=1, cb=0):
     return lax.dot_general(a, b, (((ca,), (cb,)), ((), ())), preferred_element_type=F32)
 
 
-def gelu(a):
-    t = jnp.tanh(a * (C0 + C1 * (a * a)))
-    half = 0.5 * a
+def gelu(half):
+    t = jnp.tanh(half * (H0 + H1 * (half * half)))
     return half + half * t
 
 
-def gelu_both(a):
-    a2 = a * a
-    t = jnp.tanh(a * (C0 + C1 * a2))
-    s = 0.5 + 0.5 * t
-    u = a * s
-    return u, s + u * (1.0 - s) * (2.0 * C0 + (6.0 * C1) * a2)
+def gelu_both(half):
+    sq = half * half
+    t = jnp.tanh(half * (H0 + H1 * sq))
+    s = 1.0 + t
+    u = half * s
+    return u, s + u * (1.0 - t) * (H0 + (3.0 * H1) * sq)
 
 
 def layer_forward(h_ref, w1b_ref, w2b_ref, u_ref, hs_ref, chunk, tile):
@@ -57,7 +58,7 @@
     def _():
         h_ref[...] = x_ref[...].astype(F32)
 
-    w1b_ref[...] = w1_ref[...].astype(BF16)
+    w1b_ref[...] = (0.5 * w1_ref[...]).astype(BF16)
     w2b_ref[...] = w2_ref[...].astype(BF16)
     layer_forward(h_ref, w1b_ref, w2b_ref, u_ref, hs_ref, 256, 256)
 
@@ -66,31 +67,61 @@
         g_ref[...] = (h_ref[...] - y_ref[...].astype(F32)) * scale
 
 
-def update_kernel(rate, x_ref, y_ref, w1_ref, w2_ref, m1_ref, m2_ref, gr_ref,
-                  w1o_ref, w2o_ref, m1o_ref, m2o_ref, loss_ref, h_ref, w1b_ref, w2b_ref, u_ref):
-    layer = pl.program_id(0)
-    width = w1_ref.shape[0]
-
-    @pl.when(layer == 0)
-    def _():
-        h_ref[...] = x_ref[...].astype(F32)
-
-    mom = MOMENTUM * m1_ref[...] + gr_ref[:width, :].astype(F32)
-    m1o_ref[...] = mom
-    new = w1_ref[...] - rate * mom
-    w1o_ref[...] = new
-    w1b_ref[...] = new.astype(BF16)
-    mom = MOMENTUM * m2_ref[...] + gr_ref[width:, :].astype(F32).T
-    m2o_ref[...] = mom
-    new = w2_ref[...] - rate * mom
-    w2o_ref[...] = new
-    w2b_ref[...] = new.astype(BF16)
-    layer_forward(h_ref, w1b_ref, w2b_ref, u_ref, None, 256, 256)
-
-    @pl.when(layer == pl.num_programs(0) - 1)
-    def _():
-        resid = h_ref[...] - y_ref[...].astype(F32)
-        loss_ref[...] = jnp.sum((resid * resid).T, axis=0, keepdims=True) / (2 * width)
+def update_kernel(rate, x_ref, y_ref, w1_hbm, w2_hbm, m1_hbm, m2_hbm, gr_hbm,
+                  w1o_hbm, w2o_hbm, m1o_hbm, m2o_hbm, loss_ref, h_ref,
+                  w1_ref, w2_ref, m1_ref, m2_ref, gr_ref, w1b_ref, w2b_ref, u_ref, in_sem, out_sem):
+    layers, width = w1_hbm.shape[0], w1_hbm.shape[1]
+    states = ((w1_hbm, w1_ref, w1o_hbm), (w2_hbm, w2_ref, w2o_hbm), (m1_hbm, m1_ref, m1o_hbm), (m2_hbm, m2_ref, m2o_hbm))
+
+    def reads(layer):
+        slot = layer % SLOTS
+        pairs = [(src, buf) for src, buf, _ in states] + [(gr_hbm, gr_ref)]
+        return [pltpu.make_async_copy(src.at[layer], buf.at[slot], in_sem.at[slot, n]) for n, (src, buf) in enumerate(pairs)]
+
+    def writes(layer):
+        slot = layer % SLOTS
+        return [pltpu.make_async_copy(buf.at[slot], dst.at[layer], out_sem.at[slot, n])
+                for n, (_, buf, dst) in enumerate(states)]
+
+    for layer in range(AHEAD):
+        for copy in reads(layer):
+            copy.start()
+    h_ref[...] = x_ref[...].astype(F32)
+
+    @pl.loop(0, layers)
+    def _(layer):
+        slot = layer % SLOTS
+
+        @pl.when(layer + AHEAD < layers)
+        def _():
+            @pl.when(layer + AHEAD >= SLOTS)
+            def _():
+                for copy in writes(layer + AHEAD - SLOTS):
+                    copy.wait()
+            for copy in reads(layer + AHEAD):
+                copy.start()
+
+        for copy in reads(layer):
+            copy.wait()
+        mom = MOMENTUM * m1_ref[slot] + gr_ref[slot, :width, :].astype(F32)
+        m1_ref[slot] = mom
+        new = w1_ref[slot] - rate * mom
+        w1_ref[slot] = new
+        w1b_ref[...] = (0.5 * new).astype(BF16)
+        mom = MOMENTUM * m2_ref[slot] + gr_ref[slot, width:, :].astype(F32).T
+        m2_ref[slot] = mom
+        new = w2_ref[slot] - rate * mom
+        w2_ref[slot] = new
+        w2b_ref[...] = new.astype(BF16)
+        for copy in writes(layer):
+            copy.start()
+        layer_forward(h_ref, w1b_ref, w2b_ref, u_ref, None, 256, 256)
+
+    resid = h_ref[...] - y_ref[...].astype(F32)
+    loss_ref[...] = jnp.sum((resid * resid).T, axis=0, keepdims=True) / (2 * width)
+    for layer in range(layers - SLOTS, layers):
+        for copy in writes(layer):
+            copy.wait()
 
 
 def backward_kernel(layers, g0_ref, w1_ref, w2_ref, hs_ref, out_ref,
@@ -99,13 +130,9 @@
     it = pl.program_id(0)
     pod, data = lax.axis_index("pod"), lax.axis_index("data")
     z, y, x, c = pod // 2, pod % 2, data // 2, data % 2
-    bits = {"x": x, "y": y, "z": z}
-    peers = {
-        "core": (pod, x * 2 + (1 - c)),
-        "x": (pod, (1 - x) * 2 + c),
-        "y": (z * 2 + (1 - y), data),
-        "z": ((1 - z) * 2 + y, data),
-    }
+    places = (x, y, z)
+    neighbours = ((pod, (1 - x) * 2 + c), (z * 2 + (1 - y), data), ((1 - z) * 2 + y, data))
+    sibling = (pod, x * 2 + (1 - c))
     rows, width = g_ref.shape
     hidden = u_ref.shape[1]
     block = 2 * width
@@ -116,7 +143,7 @@
     @pl.when(it == 0)
     def _():
         barrier = pltpu.get_barrier_semaphore()
-        for peer in peers.values():
+        for peer in neighbours + (sibling,):
             pl.semaphore_signal(barrier, inc=1, device_id=peer, device_id_type=MESH)
         pl.semaphore_wait(barrier, 4)
         g_ref[...] = g0_ref[...]
@@ -124,26 +151,30 @@
     def ring(slot):
         return slot % RING
 
-    def region(part, k):
+    def pick(axis, options):
+        weights = ((2 - axis) * (1 - axis) // 2, axis * (2 - axis), axis * (axis - 1) // 2)
+        return sum(weight * option for weight, option in zip(weights, options))
+
+    def axis_of(slot, part, stage):
+        return (part + slot + stage - 1) % 3
+
+    def region(slot, part, stage):
         offset = c * (block // 2)
-        for n in range(k - 1):
-            offset = offset + bits[ORDERS[part][n]] * (block >> (n + 2))
+        for n in range(1, stage + 1):
+            offset = offset + pick(axis_of(slot, part, n), places) * (block >> (n + 1))
         return offset
 
     def message(slot, m, part):
         if m in (0, 7):
-            size = block // 2
+            stage, size, cols, peer = 0, block // 2, slice(None), sibling
             mine, other = c * size, (1 - c) * size
-            cols = slice(None)
-            axis = "core"
-            stage = 0
         else:
             stage = m if m <= 3 else 7 - m
-            axis = ORDERS[part][stage - 1]
-            size = block >> (stage + 1)
-            base = region(part, stage)
-            mine, other = base + bits[axis] * size, base + (1 - bits[axis]) * size
-            cols = pl.ds(parts[part][0], parts[part][1])
+            size, cols = block >> (stage + 1), pl.ds(*parts[part])
+            axis = axis_of(slot, part, stage)
+            place, base = pick(axis, places), region(slot, part, stage - 1)
+            mine, other = base + place * size, base + (1 - place) * size
+            peer = (pick(axis, [n[0] for n in neighbours]), pick(axis, [n[1] for n in neighbours]))
         if m <= 3:
             src = grad_ref.at[ring(slot), pl.ds(pl.multiple_of(other, 16), size), cols]
             dst = recv_refs[stage].at[slot, :, cols]
@@ -152,7 +183,7 @@
             dst = src
         return pltpu.make_async_remote_copy(
             src_ref=src, dst_ref=dst, send_sem=send_sem.at[slot, m, part], recv_sem=recv_sem.at[slot, m, part],
-            device_id=peers[axis], device_id_type=MESH)
+            device_id=peer, device_id_type=MESH)
 
     def parts_of(m):
         return (0,) if m in (0, 7) else (0, 1, 2)
@@ -162,7 +193,7 @@
         if stage == 0:
             mine, cols = c * size, pl.ds(0, hidden)
         else:
-            mine, cols = region(part, stage + 1), pl.ds(*parts[part])
+            mine, cols = region(slot, part, stage), pl.ds(*parts[part])
         where = pl.ds(pl.multiple_of(mine, 16), size)
         total = grad_ref[ring(slot), where, cols].astype(F32) + recv_refs[stage][slot, :, cols].astype(F32)
         if stage == 3:
@@ -214,7 +245,7 @@
                 u_ref[r:r + chunk, cols] = u.astype(BF16)
                 q_ref[r:r + chunk, cols] = (slope * gu).astype(BF16)
             layer = layers - 1 - it
-            grad_ref[ring(layer), width:, cols] = dot(gt_ref[...], u_ref[:, cols]).astype(BF16)
+            grad_ref[ring(layer), width:, cols] = (2.0 * dot(gt_ref[...], u_ref[:, cols])).astype(BF16)
             grad_ref[ring(layer), :width, cols] = dot(ht_ref[...], q_ref[:, cols]).astype(BF16)
             for r in range(0, rows, chunk):
                 g_ref[r:r + chunk, :] = g_ref[r:r + chunk, :] + dot(q_ref[r:r + chunk, cols], w1_ref[:, cols], 1, 1)
@@ -226,12 +257,12 @@
 
     @pl.when(it == layers - 1)
     def _():
-        for tick in range(2 * layers, 2 * layers + LAGS[8] + 1):
-            for s in reversed(range(9)):
-                if (tick - LAGS[s]) % 2 == 0:
-                    done = (tick - 2 - LAGS[s]) // 2
-                    if 0 <= done < layers:
-                        step(s, layers - 1 - done)
+        taken = [sum(2 * n + 2 + lag < 2 * layers for lag in LAGS) for n in range(layers)]
+        while min(taken) < 9:
+            for n in reversed(range(layers)):
+                if taken[n] < 9:
+                    step(taken[n], layers - 1 - n)
+                    taken[n] += 1
         for slot in range(layers):
             result_copy(slot).wait()
 
@@ -253,7 +284,7 @@
         matmul_flops = 2 * rows * width * hidden * layers
 
         hs, w1b, w2b, g0 = pl.pallas_call(
-            functools.partial(forward_kernel, 1.0 / (batch * width)),
+            functools.partial(forward_kernel, 0.5 / (batch * width)),
             grid=(layers,),
             in_specs=[whole(rows, width), whole(rows, width), per_layer(width, hidden), per_layer(hidden, width)],
             out_specs=[per_layer(rows, width), per_layer(width, hidden), per_layer(hidden, width), whole(rows, width)],
@@ -296,17 +327,18 @@
 
         outs = pl.pallas_call(
             functools.partial(update_kernel, LEARN_BASE / layers),
-            grid=(layers,),
-            in_specs=[whole(rows, width), whole(rows, width), per_layer(width, hidden), per_layer(hidden, width),
-                      per_layer(width, hidden), per_layer(hidden, width), per_layer(2 * width, hidden)],
-            out_specs=[per_layer(width, hidden), per_layer(hidden, width), per_layer(width, hidden),
-                       per_layer(hidden, width), whole(1, rows), whole(rows, width)],
+            in_specs=[pl.BlockSpec(memory_space=pltpu.VMEM)] * 2 + [pl.BlockSpec(memory_space=pl.ANY)] * 5,
+            out_specs=[pl.BlockSpec(memory_space=pl.ANY)] * 4 + [pl.BlockSpec(memory_space=pltpu.VMEM)] * 2,
             out_shape=[shape((layers, width, hidden), F32), shape((layers, hidden, width), F32),
                        shape((layers, width, hidden), F32), shape((layers, hidden, width), F32),
                        shape((1, rows), F32), shape((rows, width), F32)],
-            scratch_shapes=[pltpu.VMEM((width, hidden), BF16), pltpu.VMEM((hidden, width), BF16),
-                            pltpu.VMEM((rows, hidden), BF16)],
-            compiler_params=pltpu.CompilerParams(dimension_semantics=("arbitrary",), vmem_limit_bytes=VMEM_LIMIT),
+            scratch_shapes=[pltpu.VMEM((SLOTS, width, hidden), F32), pltpu.VMEM((SLOTS, hidden, width), F32),
+                            pltpu.VMEM((SLOTS, width, hidden), F32), pltpu.VMEM((SLOTS, hidden, width), F32),
+                            pltpu.VMEM((SLOTS, 2 * width, hidden), BF16),
+                            pltpu.VMEM((width, hidden), BF16), pltpu.VMEM((hidden, width), BF16),
+                            pltpu.VMEM((rows, hidden), BF16),
+                            pltpu.SemaphoreType.DMA((SLOTS, 5)), pltpu.SemaphoreType.DMA((SLOTS, 4))],
+            compiler_params=pltpu.CompilerParams(vmem_limit_bytes=VMEM_LIMIT),
             cost_estimate=pl.CostEstimate(flops=2 * matmul_flops, bytes_accessed=160_000_000, transcendentals=0),
             name="update_forward_next",
         )(x_next, y_next, w_first, w_second, m_first, m_second, grads)

time: 256 us -> 222 us (0.87)
  Pallas kernels: 255 us -> 221 us
    pallas_call x1, Pallas kernels: 160 us -> 138 us  [train_step(): pl.pallas_call(functools.partial(backward_kernel, layers), grid=(layers,)...]
    pallas_call x2, Pallas kernels: 94.3 us -> 83 us  [the longest x1 50.6 us: train_step(): pl.pallas_call(functools.partial(update_kernel, LEARN_BASE / layers), in_...]
where the time goes in v2:
time: 222 us
  Pallas kernels  221 us (100%)
    pallas_call x1, Pallas kernels, train_step(): pl.pallas_call(functools.partial(backward_kernel, layers), grid=(layers,)...  138 us
    pallas_call x1, Pallas kernels, train_step(): pl.pallas_call(functools.partial(update_kernel, LEARN_BASE / layers), in_...  50.6 us
    pallas_call x1, Pallas kernels, train_step(): pl.pallas_call(functools.partial(forward_kernel, 0.5 / (batch * width)),...  32.4 us

profile of v2, /device:TPU:0, one launch (start us, length us, event | category | flops | bytes accessed | tf_op | source)
XLA Modules:
  0.0 221.7 jit_solution(10849293625811688296)
XLA Ops:
  0.6 32.4 %forward_now.1 = (bf16[16,1024,256]{2,1,0:T(8,128)(2,1)}, bf16[16,256,1024]{2,1,0:T(8,128)(2,1)}, bf16[16,1024,256]{2,1,0:T(8,128)(2,1)}, f32[1024,256]{1,0:T(8,128)}) custom-call(bf16[1024,256]{1,0:T(8,128)(2,1)} %x_ref.2, bf16[1024,256]{1,0:T(8,128)(2,1)} %y_ref.2, f32[16,256,1024]{2,1,0:T(8,128)} %w1_hbm.1, f32[16,1024,256]{2,1,0:T(8,128)} %w2_hbm.1), custom_call_target="tpu_custom_call" | custom-call | flops 17179869184 | bytes 60000000 | tf_op jit(solution)/shard_map/forward_now/pallas_call | solution.py:286
  33.0 138.0 %backward_reduce.1.gr_hbm = bf16[16,512,1024]{2,1,0:T(8,128)(2,1)} custom-call(f32[1024,256]{1,0:T(8,128)} %get-tuple-element.16.g0_ref, bf16[16,256,1024]{2,1,0:T(8,128)(2,1)} %get-tuple-element.17.w1_ref, bf16[16,1024,256]{2,1,0:T(8,128)(2,1)} %get-tuple-element.18.w2_ref, bf16[16,1024,256]{2,1,0:T(8,128)(2,1)} %get-tuple-element.19.hs_ref), custom_call_target="tpu_custom_call" | custom-call | flops 42949672960 | bytes 60000000 | tf_op jit(solution)/shard_map/backward_reduce/pallas_call | solution.py:299
  171.1 50.6 %update_forward_next.1 = (f32[16,256,1024]{2,1,0:T(8,128)}, f32[16,1024,256]{2,1,0:T(8,128)}, f32[16,256,1024]{2,1,0:T(8,128)}, f32[16,1024,256]{2,1,0:T(8,128)}...) custom-call(bf16[1024,256]{1,0:T(8,128)(2,1)} %x_ref.3, bf16[1024,256]{1,0:T(8,128)(2,1)} %y_ref.3, f32[16,256,1024]{2,1,0:T(8,128)} %w1_hbm.1, ...), custom_call_target="tpu_custom_call" | custom-call | flops 17179869184 | bytes 160000000 | tf_op jit(solution)/shard_map/update_forward_next/pallas_call | solution.py:328

commit v3 on v2

--- a/solution.py
+++ b/solution.py
@@ -16,11 +16,13 @@
 F32 = jnp.float32
 BF16 = jnp.bfloat16
 VMEM_LIMIT = 67_000_000
+BACK_LIMIT = 46 << 20
+UPDATE_LIMIT = 26 << 20
 
 LAGS = (0, 2, 4, 6, 7, 9, 11, 13, 15)
 RING = 6
-SLOTS = 6
-AHEAD = 4
+SLOTS = 5
+AHEAD = 3
 
 
 def dot(a, b, ca=1, cb=0):
@@ -67,15 +69,15 @@
         g_ref[...] = (h_ref[...] - y_ref[...].astype(F32)) * scale
 
 
-def update_kernel(rate, x_ref, y_ref, w1_hbm, w2_hbm, m1_hbm, m2_hbm, gr_hbm,
+def update_kernel(rate, x_ref, y_ref, w1_hbm, w2_hbm, m1_hbm, m2_hbm, gr_ref,
                   w1o_hbm, w2o_hbm, m1o_hbm, m2o_hbm, loss_ref, h_ref,
-                  w1_ref, w2_ref, m1_ref, m2_ref, gr_ref, w1b_ref, w2b_ref, u_ref, in_sem, out_sem):
+                  w1_ref, w2_ref, m1_ref, m2_ref, w1b_ref, w2b_ref, u_ref, in_sem, out_sem):
     layers, width = w1_hbm.shape[0], w1_hbm.shape[1]
     states = ((w1_hbm, w1_ref, w1o_hbm), (w2_hbm, w2_ref, w2o_hbm), (m1_hbm, m1_ref, m1o_hbm), (m2_hbm, m2_ref, m2o_hbm))
 
     def reads(layer):
         slot = layer % SLOTS
-        pairs = [(src, buf) for src, buf, _ in states] + [(gr_hbm, gr_ref)]
+        pairs = [(src, buf) for src, buf, _ in states]
         return [pltpu.make_async_copy(src.at[layer], buf.at[slot], in_sem.at[slot, n]) for n, (src, buf) in enumerate(pairs)]
 
     def writes(layer):
@@ -103,12 +105,12 @@
 
         for copy in reads(layer):
             copy.wait()
-        mom = MOMENTUM * m1_ref[slot] + gr_ref[slot, :width, :].astype(F32)
+        mom = MOMENTUM * m1_ref[slot] + gr_ref[layer, :width, :].astype(F32)
         m1_ref[slot] = mom
         new = w1_ref[slot] - rate * mom
         w1_ref[slot] = new
         w1b_ref[...] = (0.5 * new).astype(BF16)
-        mom = MOMENTUM * m2_ref[slot] + gr_ref[slot, width:, :].astype(F32).T
+        mom = MOMENTUM * m2_ref[slot] + gr_ref[layer, width:, :].astype(F32).T
         m2_ref[slot] = mom
         new = w2_ref[slot] - rate * mom
         w2_ref[slot] = new
@@ -124,10 +126,10 @@
             copy.wait()
 
 
-def backward_kernel(layers, g0_ref, w1_ref, w2_ref, hs_ref, out_ref,
+def backward_kernel(g0_ref, w1_hbm, w2_hbm, hs_hbm, sum_ref, w1_buf, w2_buf, hs_buf, in_sem,
                     g_ref, gb_ref, gt_ref, ht_ref, u_ref, q_ref,
-                    grad_ref, sum_ref, r0_ref, r1_ref, r2_ref, r3_ref, send_sem, recv_sem, out_sem):
-    it = pl.program_id(0)
+                    grad_ref, r0_ref, r1_ref, r2_ref, r3_ref, send_sem, recv_sem):
+    layers = w1_hbm.shape[0]
     pod, data = lax.axis_index("pod"), lax.axis_index("data")
     z, y, x, c = pod // 2, pod % 2, data // 2, data % 2
     places = (x, y, z)
@@ -140,13 +142,18 @@
     third = hidden // 128 * 3 // 8 * 128
     parts = ((0, third), (third, third), (2 * third, hidden - 2 * third))
 
-    @pl.when(it == 0)
-    def _():
-        barrier = pltpu.get_barrier_semaphore()
-        for peer in neighbours + (sibling,):
-            pl.semaphore_signal(barrier, inc=1, device_id=peer, device_id_type=MESH)
-        pl.semaphore_wait(barrier, 4)
-        g_ref[...] = g0_ref[...]
+    def reads(it):
+        slot, layer = it % 2, layers - 1 - it
+        pairs = ((w1_hbm, w1_buf), (w2_hbm, w2_buf), (hs_hbm, hs_buf))
+        return [pltpu.make_async_copy(src.at[layer], buf.at[slot], in_sem.at[slot, n]) for n, (src, buf) in enumerate(pairs)]
+
+    for copy in reads(0):
+        copy.start()
+    barrier = pltpu.get_barrier_semaphore()
+    for peer in neighbours + (sibling,):
+        pl.semaphore_signal(barrier, inc=1, device_id=peer, device_id_type=MESH)
+    pl.semaphore_wait(barrier, 4)
+    g_ref[...] = g0_ref[...]
 
     def ring(slot):
         return slot % RING
@@ -201,9 +208,6 @@
         else:
             grad_ref[ring(slot), where, cols] = total.astype(BF16)
 
-    def result_copy(slot):
-        return pltpu.make_async_copy(sum_ref.at[slot], out_ref.at[slot], out_sem.at[slot])
-
     def step(s, slot):
         if s > 0:
             m = s - 1
@@ -216,10 +220,8 @@
         if s == 0 or s == 1 or s == 7:
             for part in parts_of(s):
                 message(slot, s, part).start()
-        if s == 8:
-            result_copy(slot).start()
-
-    def comm_point(parity):
+
+    def comm_point(it, parity):
         for s in reversed(range(9)):
             if LAGS[s] % 2 == parity:
                 done = it - 1 - (LAGS[s] - parity) // 2
@@ -229,42 +231,69 @@
                     step(s, layers - 1 - done)
 
     tile, chunk = 256, 256
-    comm_point(0)
-
-    gb_ref[...] = g_ref[...].astype(BF16)
-    gt_ref[...] = gb_ref[...].T
-    ht_ref[...] = hs_ref[...].T
-
-    def half(tiles):
-        for n in tiles:
+
+    @pl.loop(0, layers)
+    def _(it):
+        comm_point(it, 0)
+
+        @pl.when(it + 1 < layers)
+        def _():
+            for copy in reads(it + 1):
+                copy.start()
+
+        for copy in reads(it):
+            copy.wait()
+        w1_ref, w2_ref, hs_ref = (buf.at[it % 2] for buf in (w1_buf, w2_buf, hs_buf))
+
+        gb_ref[...] = g_ref[...].astype(BF16)
+        gt_ref[...] = gb_ref[...].T
+        ht_ref[...] = hs_ref[...].T
+
+        layer = layers - 1 - it
+
+        def first(n, r):
             cols = slice(n, n + tile)
-            for r in range(0, rows, chunk):
-                a = dot(hs_ref[r:r + chunk, :], w1_ref[:, cols])
-                gu = dot(gb_ref[r:r + chunk, :], w2_ref[cols, :], 1, 1)
-                u, slope = gelu_both(a)
-                u_ref[r:r + chunk, cols] = u.astype(BF16)
-                q_ref[r:r + chunk, cols] = (slope * gu).astype(BF16)
-            layer = layers - 1 - it
+            a = dot(hs_ref[r:r + chunk, :], w1_ref[:, cols])
+            gu = dot(gb_ref[r:r + chunk, :], w2_ref[cols, :], 1, 1)
+            u, slope = gelu_both(a)
+            u_ref[r:r + chunk, cols] = u.astype(BF16)
+            q_ref[r:r + chunk, cols] = (slope * gu).astype(BF16)
+
+        def carry(n, r):
+            cols = slice(n, n + tile)
+            g_ref[r:r + chunk, :] = g_ref[r:r + chunk, :] + dot(q_ref[r:r + chunk, cols], w1_ref[:, cols], 1, 1)
+
+        def grad_second(n):
+            cols = slice(n, n + tile)
             grad_ref[ring(layer), width:, cols] = (2.0 * dot(gt_ref[...], u_ref[:, cols])).astype(BF16)
+
+        def grad_first(n):
+            cols = slice(n, n + tile)
             grad_ref[ring(layer), :width, cols] = dot(ht_ref[...], q_ref[:, cols]).astype(BF16)
-            for r in range(0, rows, chunk):
-                g_ref[r:r + chunk, :] = g_ref[r:r + chunk, :] + dot(q_ref[r:r + chunk, cols], w1_ref[:, cols], 1, 1)
-
-    tiles = list(range(0, hidden, tile))
-    half(tiles[:len(tiles) // 2])
-    comm_point(1)
-    half(tiles[len(tiles) // 2:])
-
-    @pl.when(it == layers - 1)
-    def _():
-        taken = [sum(2 * n + 2 + lag < 2 * layers for lag in LAGS) for n in range(layers)]
-        while min(taken) < 9:
-            for n in reversed(range(layers)):
-                if taken[n] < 9:
-                    step(taken[n], layers - 1 - n)
-                    taken[n] += 1
-        for slot in range(layers):
-            result_copy(slot).wait()
+
+        def tile_step(n, previous):
+            for i, r in enumerate(range(0, rows, chunk)):
+                if previous is not None:
+                    carry(previous, r)
+                    if i == rows // chunk // 2 - 1:
+                        grad_second(previous)
+                if n is not None:
+                    first(n, r)
+            if previous is not None:
+                grad_first(previous)
+
+        tiles = list(range(0, hidden, tile)) + [None]
+        for i, n in enumerate(tiles):
+            if i == len(tiles) // 2:
+                comm_point(it, 1)
+            tile_step(n, tiles[i - 1] if i > 0 else None)
+
+    taken = [sum(2 * n + 2 + lag < 2 * layers for lag in LAGS) for n in range(layers)]
+    while min(taken) < 9:
+        for n in reversed(range(layers)):
+            if taken[n] < 9:
+                step(taken[n], layers - 1 - n)
+                taken[n] += 1
 
 
 def solution(mesh):
@@ -279,7 +308,6 @@
         batch = rows * n_pod * n_data
         whole = lambda *shape: pl.BlockSpec(shape, lambda i: (0,) * len(shape))
         per_layer = lambda *shape: pl.BlockSpec((None,) + shape, lambda i: (i, 0, 0))
-        reverse = lambda *shape: pl.BlockSpec((None,) + shape, lambda i: (layers - 1 - i, 0, 0))
         shape = jax.ShapeDtypeStruct
         matmul_flops = 2 * rows * width * hidden * layers
 
@@ -297,12 +325,15 @@
         )(x_now, y_now, w_first, w_second)
 
         grads = pl.pallas_call(
-            functools.partial(backward_kernel, layers),
-            grid=(layers,),
-            in_specs=[whole(rows, width), reverse(width, hidden), reverse(hidden, width), reverse(rows, width)],
-            out_specs=pl.BlockSpec(memory_space=pl.ANY),
-            out_shape=shape((layers, 2 * width, hidden), BF16),
+            backward_kernel,
+            in_specs=[pl.BlockSpec(memory_space=pltpu.VMEM)] + [pl.BlockSpec(memory_space=pl.ANY)] * 3,
+            out_specs=pl.BlockSpec(memory_space=pltpu.VMEM),
+            out_shape=pltpu.VMEM((layers, 2 * width, hidden), BF16),
             scratch_shapes=[
+                pltpu.VMEM((2, width, hidden), BF16),
+                pltpu.VMEM((2, hidden, width), BF16),
+                pltpu.VMEM((2, rows, width), BF16),
+                pltpu.SemaphoreType.DMA((2, 3)),
                 pltpu.VMEM((rows, width), F32),
                 pltpu.VMEM((rows, width), BF16),
                 pltpu.VMEM((width, rows), BF16),
@@ -310,16 +341,14 @@
                 pltpu.VMEM((rows, hidden), BF16),
                 pltpu.VMEM((rows, hidden), BF16),
                 pltpu.VMEM((RING, 2 * width, hidden), BF16),
-                pltpu.VMEM((layers, 2 * width, hidden), BF16),
                 pltpu.VMEM((layers, width, hidden), BF16),
                 pltpu.VMEM((layers, width // 2, hidden), BF16),
                 pltpu.VMEM((layers, width // 4, hidden), BF16),
                 pltpu.VMEM((layers, width // 8, hidden), BF16),
                 pltpu.SemaphoreType.DMA((layers, 8, 3)),
                 pltpu.SemaphoreType.DMA((layers, 8, 3)),
-                pltpu.SemaphoreType.DMA((layers,)),
             ],
-            compiler_params=pltpu.CompilerParams(dimension_semantics=("arbitrary",), vmem_limit_bytes=VMEM_LIMIT,
+            compiler_params=pltpu.CompilerParams(vmem_limit_bytes=BACK_LIMIT,
                                                  collective_id=0, has_side_effects=True),
             cost_estimate=pl.CostEstimate(flops=5 * matmul_flops, bytes_accessed=60_000_000, transcendentals=0),
             name="backward_reduce",
@@ -327,21 +356,21 @@
 
         outs = pl.pallas_call(
             functools.partial(update_kernel, LEARN_BASE / layers),
-            in_specs=[pl.BlockSpec(memory_space=pltpu.VMEM)] * 2 + [pl.BlockSpec(memory_space=pl.ANY)] * 5,
+            in_specs=[pl.BlockSpec(memory_space=pltpu.VMEM)] * 2 + [pl.BlockSpec(memory_space=pl.ANY)] * 4 +
+                     [pl.BlockSpec(memory_space=pltpu.VMEM)],
             out_specs=[pl.BlockSpec(memory_space=pl.ANY)] * 4 + [pl.BlockSpec(memory_space=pltpu.VMEM)] * 2,
             out_shape=[shape((layers, width, hidden), F32), shape((layers, hidden, width), F32),
                        shape((layers, width, hidden), F32), shape((layers, hidden, width), F32),
                        shape((1, rows), F32), shape((rows, width), F32)],
             scratch_shapes=[pltpu.VMEM((SLOTS, width, hidden), F32), pltpu.VMEM((SLOTS, hidden, width), F32),
                             pltpu.VMEM((SLOTS, width, hidden), F32), pltpu.VMEM((SLOTS, hidden, width), F32),
-                            pltpu.VMEM((SLOTS, 2 * width, hidden), BF16),
                             pltpu.VMEM((width, hidden), BF16), pltpu.VMEM((hidden, width), BF16),
                             pltpu.VMEM((rows, hidden), BF16),
-                            pltpu.SemaphoreType.DMA((SLOTS, 5)), pltpu.SemaphoreType.DMA((SLOTS, 4))],
-            compiler_params=pltpu.CompilerParams(vmem_limit_bytes=VMEM_LIMIT),
+                            pltpu.SemaphoreType.DMA((SLOTS, 4)), pltpu.SemaphoreType.DMA((SLOTS, 4))],
+            compiler_params=pltpu.CompilerParams(vmem_limit_bytes=UPDATE_LIMIT),
             cost_estimate=pl.CostEstimate(flops=2 * matmul_flops, bytes_accessed=160_000_000, transcendentals=0),
             name="update_forward_next",
-        )(x_next, y_next, w_first, w_second, m_first, m_second, grads)
+        )(x_next, y_next, w_first, w_second, m_first, m_second, pltpu.with_memory_space_constraint(grads, pltpu.VMEM))
         return outs[0], outs[1], outs[2], outs[3], outs[4].reshape(rows), outs[5]
 
     return jax.shard_map(train_step, mesh=mesh,

time: 222 us -> 216 us (0.973)
  Pallas kernels: 221 us -> 215 us
    pallas_call x1, Pallas kernels: 50.6 us -> 46.2 us  [train_step(): pl.pallas_call(functools.partial(update_kernel, LEARN_BASE / layers), in_...]
where the time goes in v3:
time: 216 us
  Pallas kernels  215 us (100%)
    pallas_call x1, Pallas kernels, train_step(): pl.pallas_call(backward_kernel, in_specs=[pl.BlockSpec(memory_space=pltpu...  136 us
    pallas_call x1, Pallas kernels, train_step(): pl.pallas_call(functools.partial(update_kernel, LEARN_BASE / layers), in_...  46.2 us
    pallas_call x1, Pallas kernels, train_step(): pl.pallas_call(functools.partial(forward_kernel, 0.5 / (batch * width)),...  32.4 us

profile of v3, /device:TPU:0, one launch (start us, length us, event | category | flops | bytes accessed | tf_op | source)
XLA Modules:
  0.0 215.7 jit_solution(11482762375609790054)
XLA Ops:
  0.6 32.4 %forward_now.1 = (bf16[16,1024,256]{2,1,0:T(8,128)(2,1)}, bf16[16,256,1024]{2,1,0:T(8,128)(2,1)}, bf16[16,1024,256]{2,1,0:T(8,128)(2,1)}, f32[1024,256]{1,0:T(8,128)}) custom-call(bf16[1024,256]{1,0:T(8,128)(2,1)} %x_ref.2, bf16[1024,256]{1,0:T(8,128)(2,1)} %y_ref.2, f32[16,256,1024]{2,1,0:T(8,128)} %w1_hbm.1, f32[16,1024,256]{2,1,0:T(8,128)} %w2_hbm.1), custom_call_target="tpu_custom_call" | custom-call | flops 17179869184 | bytes 60000000 | tf_op jit(solution)/shard_map/forward_now/pallas_call | solution.py:314
  33.0 0.0 copy-start
  33.0 0.0 copy-start.1
  33.0 136.4 %backward_reduce.1.gr_ref = bf16[16,512,1024]{2,1,0:T(8,128)(2,1)S(1)} custom-call(f32[1024,256]{1,0:T(8,128)} %get-tuple-element.16.g0_ref, bf16[16,256,1024]{2,1,0:T(8,128)(2,1)} %get-tuple-element.17.w1_hbm, bf16[16,1024,256]{2,1,0:T(8,128)(2,1)} %get-tuple-element.18.w2_hbm, bf16[16,1024,256]{2,1,0:T(8,128)(2,1)} %get-tuple-element.19.hs_hbm), custom_call_target="tpu_custom_call" | custom-call | flops 42949672960 | bytes 60000000 | tf_op jit(solution)/shard_map/backward_reduce/pallas_call | solution.py:327
  169.5 0.0 copy-done
  169.5 0.0 copy-done.1
  169.5 46.2 %update_forward_next.1 = (f32[16,256,1024]{2,1,0:T(8,128)}, f32[16,1024,256]{2,1,0:T(8,128)}, f32[16,256,1024]{2,1,0:T(8,128)}, f32[16,1024,256]{2,1,0:T(8,128)}...) custom-call(bf16[1024,256]{1,0:T(8,128)(2,1)S(1)} %copy-done, bf16[1024,256]{1,0:T(8,128)(2,1)S(1)} %copy-done.1, ...), custom_call_target="tpu_custom_call" | custom-call | flops 17179869184 | bytes 160000000 | tf_op jit(solution)/shard_map/update_forward_next/pallas_call | solution.py:357
Async XLA Ops:
  33.0 136.5 %copy-start = (bf16[1024,256]{1,0:T(8,128)(2,1)S(1)}, bf16[1024,256]{1,0:T(8,128)(2,1)}, u32[]{:S(2)}) copy-start(bf16[1024,256]{1,0:T(8,128)(2,1)} %x_ref.3) | copy-start | bytes 1572868
  33.0 136.5 %copy-start.1 = (bf16[1024,256]{1,0:T(8,128)(2,1)S(1)}, bf16[1024,256]{1,0:T(8,128)(2,1)}, u32[]{:S(2)}) copy-start(bf16[1024,256]{1,0:T(8,128)(2,1)} %y_ref.3) | copy-start | bytes 1572868

commit v4 on v3

--- a/solution.py
+++ b/solution.py
@@ -15,10 +15,10 @@
 MESH = pl.DeviceIdType.MESH
 F32 = jnp.float32
 BF16 = jnp.bfloat16
-VMEM_LIMIT = 67_000_000
 BACK_LIMIT = 46 << 20
 UPDATE_LIMIT = 26 << 20
 
+LOADS = 3
 LAGS = (0, 2, 4, 6, 7, 9, 11, 13, 15)
 RING = 6
 SLOTS = 5
@@ -51,22 +51,6 @@
         for n in range(0, width, tile):
             u_ref[r:r + chunk, n:n + tile] = gelu(dot(hb, w1b_ref[:, n:n + tile])).astype(BF16)
         h_ref[r:r + chunk, :] = h_ref[r:r + chunk, :] + dot(u_ref[r:r + chunk, :], w2b_ref[...])
-
-
-def forward_kernel(scale, x_ref, y_ref, w1_ref, w2_ref, hs_ref, w1b_ref, w2b_ref, g_ref, h_ref, u_ref):
-    layer = pl.program_id(0)
-
-    @pl.when(layer == 0)
-    def _():
-        h_ref[...] = x_ref[...].astype(F32)
-
-    w1b_ref[...] = (0.5 * w1_ref[...]).astype(BF16)
-    w2b_ref[...] = w2_ref[...].astype(BF16)
-    layer_forward(h_ref, w1b_ref, w2b_ref, u_ref, hs_ref, 256, 256)
-
-    @pl.when(layer == pl.num_programs(0) - 1)
-    def _():
-        g_ref[...] = (h_ref[...] - y_ref[...].astype(F32)) * scale
 
 
 def update_kernel(rate, x_ref, y_ref, w1_hbm, w2_hbm, m1_hbm, m2_hbm, gr_ref,
@@ -117,7 +101,7 @@
         w2b_ref[...] = new.astype(BF16)
         for copy in writes(layer):
             copy.start()
-        layer_forward(h_ref, w1b_ref, w2b_ref, u_ref, None, 256, 256)
+        layer_forward(h_ref, w1b_ref, w2b_ref, u_ref, None, 512, 256)
 
     resid = h_ref[...] - y_ref[...].astype(F32)
     loss_ref[...] = jnp.sum((resid * resid).T, axis=0, keepdims=True) / (2 * width)
@@ -126,10 +110,10 @@
             copy.wait()
 
 
-def backward_kernel(g0_ref, w1_hbm, w2_hbm, hs_hbm, sum_ref, w1_buf, w2_buf, hs_buf, in_sem,
-                    g_ref, gb_ref, gt_ref, ht_ref, u_ref, q_ref,
+def gradient_kernel(scale, x_ref, y_ref, w1f_hbm, w2f_hbm, sum_ref, w1_hbm, w2_hbm, hs_hbm,
+                    w1f_buf, w2f_buf, w1_buf, w2_buf, hs_buf, load_sem, save_sem, in_sem, g_ref, gb_ref, gt_ref, ht_ref, u_ref, q_ref,
                     grad_ref, r0_ref, r1_ref, r2_ref, r3_ref, send_sem, recv_sem):
-    layers = w1_hbm.shape[0]
+    layers = w1f_hbm.shape[0]
     pod, data = lax.axis_index("pod"), lax.axis_index("data")
     z, y, x, c = pod // 2, pod % 2, data // 2, data % 2
     places = (x, y, z)
@@ -142,18 +126,56 @@
     third = hidden // 128 * 3 // 8 * 128
     parts = ((0, third), (third, third), (2 * third, hidden - 2 * third))
 
-    def reads(it):
-        slot, layer = it % 2, layers - 1 - it
-        pairs = ((w1_hbm, w1_buf), (w2_hbm, w2_buf), (hs_hbm, hs_buf))
-        return [pltpu.make_async_copy(src.at[layer], buf.at[slot], in_sem.at[slot, n]) for n, (src, buf) in enumerate(pairs)]
-
-    for copy in reads(0):
-        copy.start()
+    saved = ((w1_hbm, w1_buf), (w2_hbm, w2_buf), (hs_hbm, hs_buf))
+
+    def loads(layer):
+        slot = layer % LOADS
+        return [pltpu.make_async_copy(src.at[layer], buf.at[slot], load_sem.at[slot, n])
+                for n, (src, buf) in enumerate(((w1f_hbm, w1f_buf), (w2f_hbm, w2f_buf)))]
+
+    def saves(layer):
+        slot = layer % 2
+        return [pltpu.make_async_copy(buf.at[slot], dst.at[layer], save_sem.at[slot, n]) for n, (dst, buf) in enumerate(saved)]
+
+    def reads(layer):
+        slot = layer % 2
+        return [pltpu.make_async_copy(src.at[layer], buf.at[slot], in_sem.at[slot, n]) for n, (src, buf) in enumerate(saved)]
+
+    for layer in range(LOADS - 1):
+        for copy in loads(layer):
+            copy.start()
     barrier = pltpu.get_barrier_semaphore()
     for peer in neighbours + (sibling,):
         pl.semaphore_signal(barrier, inc=1, device_id=peer, device_id_type=MESH)
+    g_ref[...] = x_ref[...].astype(F32)
+
+    @pl.loop(0, layers)
+    def _(layer):
+        slot = layer % 2
+
+        @pl.when(layer + LOADS - 1 < layers)
+        def _():
+            for copy in loads(layer + LOADS - 1):
+                copy.start()
+
+        @pl.when(layer >= 2)
+        def _():
+            for copy in saves(layer - 2):
+                copy.wait()
+
+        for copy in loads(layer):
+            copy.wait()
+        w1_buf[slot] = (0.5 * w1f_buf[layer % LOADS]).astype(BF16)
+        w2_buf[slot] = w2f_buf[layer % LOADS].astype(BF16)
+        layer_forward(g_ref, w1_buf.at[slot], w2_buf.at[slot], u_ref, hs_buf.at[slot], 512, 256)
+
+        @pl.when(layer < layers - 2)
+        def _():
+            for copy in saves(layer):
+                copy.start()
+
+    g_ref[...] = (g_ref[...] - y_ref[...].astype(F32)) * scale
     pl.semaphore_wait(barrier, 4)
-    g_ref[...] = g0_ref[...]
 
     def ring(slot):
         return slot % RING
@@ -236,20 +258,23 @@
     def _(it):
         comm_point(it, 0)
 
-        @pl.when(it + 1 < layers)
-        def _():
-            for copy in reads(it + 1):
+        layer = layers - 1 - it
+
+        @pl.when((it >= 1) & (it + 1 < layers))
+        def _():
+            for copy in reads(layer - 1):
                 copy.start()
 
-        for copy in reads(it):
-            copy.wait()
-        w1_ref, w2_ref, hs_ref = (buf.at[it % 2] for buf in (w1_buf, w2_buf, hs_buf))
+        @pl.when(it >= 2)
+        def _():
+            for copy in reads(layer):
+                copy.wait()
+
+        w1_ref, w2_ref, hs_ref = (buf.at[layer % 2] for buf in (w1_buf, w2_buf, hs_buf))
 
         gb_ref[...] = g_ref[...].astype(BF16)
         gt_ref[...] = gb_ref[...].T
         ht_ref[...] = hs_ref[...].T
-
-        layer = layers - 1 - it
 
         def first(n, r):
             cols = slice(n, n + tile)
@@ -306,33 +331,23 @@
         layers, width, hidden = w_first.shape
         rows = x_now.shape[0]
         batch = rows * n_pod * n_data
-        whole = lambda *shape: pl.BlockSpec(shape, lambda i: (0,) * len(shape))
-        per_layer = lambda *shape: pl.BlockSpec((None,) + shape, lambda i: (i, 0, 0))
         shape = jax.ShapeDtypeStruct
         matmul_flops = 2 * rows * width * hidden * layers
 
-        hs, w1b, w2b, g0 = pl.pallas_call(
-            functools.partial(forward_kernel, 0.5 / (batch * width)),
-            grid=(layers,),
-            in_specs=[whole(rows, width), whole(rows, width), per_layer(width, hidden), per_layer(hidden, width)],
-            out_specs=[per_layer(rows, width), per_layer(width, hidden), per_layer(hidden, width), whole(rows, width)],
-            out_shape=[shape((layers, rows, width), BF16), shape((layers, width, hidden), BF16),
-                       shape((layers, hidden, width), BF16), shape((rows, width), F32)],
-            scratch_shapes=[pltpu.VMEM((rows, width), F32), pltpu.VMEM((rows, hidden), BF16)],
-            compiler_params=pltpu.CompilerParams(dimension_semantics=("arbitrary",), vmem_limit_bytes=VMEM_LIMIT),
-            cost_estimate=pl.CostEstimate(flops=2 * matmul_flops, bytes_accessed=60_000_000, transcendentals=0),
-            name="forward_now",
-        )(x_now, y_now, w_first, w_second)
-
         grads = pl.pallas_call(
-            backward_kernel,
-            in_specs=[pl.BlockSpec(memory_space=pltpu.VMEM)] + [pl.BlockSpec(memory_space=pl.ANY)] * 3,
-            out_specs=pl.BlockSpec(memory_space=pltpu.VMEM),
-            out_shape=pltpu.VMEM((layers, 2 * width, hidden), BF16),
+            functools.partial(gradient_kernel, 0.5 / (batch * width)),
+            in_specs=[pl.BlockSpec(memory_space=pltpu.VMEM)] * 2 + [pl.BlockSpec(memory_space=pl.ANY)] * 2,
+            out_specs=[pl.BlockSpec(memory_space=pltpu.VMEM)] + [pl.BlockSpec(memory_space=pl.ANY)] * 3,
+            out_shape=[pltpu.VMEM((layers, 2 * width, hidden), BF16), shape((layers - 2, width, hidden), BF16),
+                       shape((layers - 2, hidden, width), BF16), shape((layers - 2, rows, width), BF16)],
             scratch_shapes=[
+                pltpu.VMEM((LOADS, width, hidden), F32),
+                pltpu.VMEM((LOADS, hidden, width), F32),
                 pltpu.VMEM((2, width, hidden), BF16),
                 pltpu.VMEM((2, hidden, width), BF16),
                 pltpu.VMEM((2, rows, width), BF16),
+                pltpu.SemaphoreType.DMA((LOADS, 2)),
+                pltpu.SemaphoreType.DMA((2, 3)),
                 pltpu.SemaphoreType.DMA((2, 3)),
                 pltpu.VMEM((rows, width), F32),
                 pltpu.VMEM((rows, width), BF16),
@@ -350,9 +365,9 @@
             ],
             compiler_params=pltpu.CompilerParams(vmem_limit_bytes=BACK_LIMIT,
                                                  collective_id=0, has_side_effects=True),
-            cost_estimate=pl.CostEstimate(flops=5 * matmul_flops, bytes_accessed=60_000_000, transcendentals=0),
-            name="backward_reduce",
-        )(g0, w1b, w2b, hs)
+            cost_estimate=pl.CostEstimate(flops=7 * matmul_flops, bytes_accessed=80_000_000, transcendentals=0),
+            name="gradient",
+        )(x_now, y_now, w_first, w_second)[0]
 
         outs = pl.pallas_call(
             functools.partial(update_kernel, LEARN_BASE / layers),

time: 216 us -> 208 us (0.963)
  Pallas kernels: 215 us -> 207 us
    pallas_call x2 -> x1, Pallas kernels: 169 us -> 161 us  [train_step(): pl.pallas_call(functools.partial(gradient_kernel, 0.5 / (batch * width)),...]
where the time goes in v4:
time: 208 us; the launch traced here: 207 us
  Pallas kernels  207 us (100%)
    pallas_call x1, Pallas kernels, train_step(): pl.pallas_call(functools.partial(gradient_kernel, 0.5 / (batch * width)),...  161 us
    pallas_call x1, Pallas kernels, train_step(): pl.pallas_call(functools.partial(update_kernel, LEARN_BASE / layers), in_...  45.1 us

profile of v4, /device:TPU:0, one launch (start us, length us, event | category | flops | bytes accessed | tf_op | source)
XLA Modules:
  0.0 207.2 jit_solution(2477076303973588659)
XLA Ops:
  0.6 0.0 copy-start.1
  0.6 0.0 copy-start
  0.7 161.5 %gradient.1 = (bf16[16,512,1024]{2,1,0:T(8,128)(2,1)S(1)}, bf16[14,256,1024]{2,1,0:T(8,128)(2,1)}, bf16[14,1024,256]{2,1,0:T(8,128)(2,1)}, bf16[14,1024,256]{2,1,0:T(8,128)(2,1)}) custom-call(bf16[1024,256]{1,0:T(8,128)(2,1)} %x_ref.2, bf16[1024,256]{1,0:T(8,128)(2,1)} %y_ref.2, f32[16,256,1024]{2,1,0:T(8,128)} %w1_hbm.1, f32[16,1024,256]{2,1,0:T(8,128)} %w2_hbm.1), custom_call_target="tpu_custom_call" | custom-call | flops 60129542144 | bytes 80000000 | tf_op jit(solution)/shard_map/gradient/pallas_call | solution.py:337
  162.1 0.0 copy-done.1
  162.1 0.0 copy-done
  162.1 45.1 %update_forward_next.1 = (f32[16,256,1024]{2,1,0:T(8,128)}, f32[16,1024,256]{2,1,0:T(8,128)}, f32[16,256,1024]{2,1,0:T(8,128)}, f32[16,1024,256]{2,1,0:T(8,128)}...) custom-call(bf16[1024,256]{1,0:T(8,128)(2,1)S(1)} %copy-done, bf16[1024,256]{1,0:T(8,128)(2,1)S(1)} %copy-done.1, ...), custom_call_target="tpu_custom_call" | custom-call | flops 17179869184 | bytes 160000000 | tf_op jit(solution)/shard_map/update_forward_next/pallas_call | solution.py:372
Async XLA Ops:
  0.6 161.5 %copy-start.1 = (bf16[1024,256]{1,0:T(8,128)(2,1)S(1)}, bf16[1024,256]{1,0:T(8,128)(2,1)}, u32[]{:S(2)}) copy-start(bf16[1024,256]{1,0:T(8,128)(2,1)} %y_ref.3) | copy-start | bytes 1572868
  0.6 161.5 %copy-start = (bf16[1024,256]{1,0:T(8,128)(2,1)S(1)}, bf16[1024,256]{1,0:T(8,128)(2,1)}, u32[]{:S(2)}) copy-start(bf16[1024,256]{1,0:T(8,128)(2,1)} %x_ref.3) | copy-start | bytes 1572868

commit v5 on v4

--- a/solution.py
+++ b/solution.py
@@ -94,11 +94,13 @@
         new = w1_ref[slot] - rate * mom
         w1_ref[slot] = new
         w1b_ref[...] = (0.5 * new).astype(BF16)
-        mom = MOMENTUM * m2_ref[slot] + gr_ref[layer, width:, :].astype(F32).T
-        m2_ref[slot] = mom
-        new = w2_ref[slot] - rate * mom
-        w2_ref[slot] = new
-        w2b_ref[...] = new.astype(BF16)
+        for n in range(0, w2_ref.shape[1], width):
+            part = slice(n, n + width)
+            mom = MOMENTUM * m2_ref[slot, part, :] + gr_ref[layer, width:, part].astype(F32)
+            m2_ref[slot, part, :] = mom
+            new = w2_ref[slot, part, :] - rate * mom
+            w2_ref[slot, part, :] = new
+            w2b_ref[part, :] = new.astype(BF16)
         for copy in writes(layer):
             copy.start()
         layer_forward(h_ref, w1b_ref, w2b_ref, u_ref, None, 512, 256)
@@ -167,7 +169,7 @@
             copy.wait()
         w1_buf[slot] = (0.5 * w1f_buf[layer % LOADS]).astype(BF16)
         w2_buf[slot] = w2f_buf[layer % LOADS].astype(BF16)
-        layer_forward(g_ref, w1_buf.at[slot], w2_buf.at[slot], u_ref, hs_buf.at[slot], 512, 256)
+        layer_forward(g_ref, w1_buf.at[slot], w2_buf.at[slot], u_ref, hs_buf.at[slot], 1024, 256)
 
         @pl.when(layer < layers - 2)
         def _():
@@ -180,32 +182,32 @@
     def ring(slot):
         return slot % RING
 
-    def pick(axis, options):
-        weights = ((2 - axis) * (1 - axis) // 2, axis * (2 - axis), axis * (axis - 1) // 2)
-        return sum(weight * option for weight, option in zip(weights, options))
-
-    def axis_of(slot, part, stage):
-        return (part + slot + stage - 1) % 3
-
-    def region(slot, part, stage):
-        offset = c * (block // 2)
-        for n in range(1, stage + 1):
-            offset = offset + pick(axis_of(slot, part, n), places) * (block >> (n + 1))
-        return offset
-
-    def message(slot, m, part):
+    def context(slot):
+        if isinstance(slot, int):
+            turn = [(slot + k) % 3 for k in range(3)]
+            return slot, slot % RING, [places[k] for k in turn], [neighbours[k] for k in turn]
+        start = slot % 3
+        first = ((2 - start) * (1 - start) // 2, start * (2 - start), start * (start - 1) // 2)
+        turned = [[sum(first[b] * values[(b + k) % 3] for b in range(3)) for k in range(3)]
+                  for values in (places, [n[0] for n in neighbours], [n[1] for n in neighbours])]
+        return slot, slot % RING, turned[0], list(zip(turned[1], turned[2]))
+
+    def region(ctx, part, stage):
+        return sum([ctx[2][(part + n - 1) % 3] * (block >> (n + 1)) for n in range(1, stage + 1)], c * (block // 2))
+
+    def message(ctx, m, part):
+        slot, kept, bits, peers = ctx
         if m in (0, 7):
             stage, size, cols, peer = 0, block // 2, slice(None), sibling
             mine, other = c * size, (1 - c) * size
         else:
             stage = m if m <= 3 else 7 - m
             size, cols = block >> (stage + 1), pl.ds(*parts[part])
-            axis = axis_of(slot, part, stage)
-            place, base = pick(axis, places), region(slot, part, stage - 1)
-            mine, other = base + place * size, base + (1 - place) * size
-            peer = (pick(axis, [n[0] for n in neighbours]), pick(axis, [n[1] for n in neighbours]))
+            axis = (part + stage - 1) % 3
+            base, peer = region(ctx, part, stage - 1), peers[axis]
+            mine, other = base + bits[axis] * size, base + (1 - bits[axis]) * size
         if m <= 3:
-            src = grad_ref.at[ring(slot), pl.ds(pl.multiple_of(other, 16), size), cols]
+            src = grad_ref.at[kept, pl.ds(pl.multiple_of(other, 16), size), cols]
             dst = recv_refs[stage].at[slot, :, cols]
         else:
             src = sum_ref.at[slot, pl.ds(pl.multiple_of(mine, 16), size), cols]
@@ -217,31 +219,33 @@
     def parts_of(m):
         return (0,) if m in (0, 7) else (0, 1, 2)
 
-    def accumulate(slot, stage, part):
+    def accumulate(ctx, stage, part):
+        slot, kept = ctx[:2]
         size = block >> (stage + 1)
         if stage == 0:
             mine, cols = c * size, pl.ds(0, hidden)
         else:
-            mine, cols = region(slot, part, stage), pl.ds(*parts[part])
+            mine, cols = region(ctx, part, stage), pl.ds(*parts[part])
         where = pl.ds(pl.multiple_of(mine, 16), size)
-        total = grad_ref[ring(slot), where, cols].astype(F32) + recv_refs[stage][slot, :, cols].astype(F32)
+        total = grad_ref[kept, where, cols].astype(F32) + recv_refs[stage][slot, :, cols].astype(F32)
         if stage == 3:
             sum_ref[slot, where, cols] = total.astype(BF16)
         else:
-            grad_ref[ring(slot), where, cols] = total.astype(BF16)
+            grad_ref[kept, where, cols] = total.astype(BF16)
 
     def step(s, slot):
+        ctx = context(slot)
         if s > 0:
             m = s - 1
             for part in parts_of(m):
-                message(slot, m, part).wait()
+                message(ctx, m, part).wait()
                 if m <= 3:
-                    accumulate(slot, m, part)
+                    accumulate(ctx, m, part)
                 if m not in (0, 7) and s < 8 and s != 7:
-                    message(slot, s, part).start()
+                    message(ctx, s, part).start()
         if s == 0 or s == 1 or s == 7:
             for part in parts_of(s):
-                message(slot, s, part).start()
+                message(ctx, s, part).start()
 
     def comm_point(it, parity):
         for s in reversed(range(9)):
@@ -290,7 +294,7 @@
 
         def grad_second(n):
             cols = slice(n, n + tile)
-            grad_ref[ring(layer), width:, cols] = (2.0 * dot(gt_ref[...], u_ref[:, cols])).astype(BF16)
+            grad_ref[ring(layer), width:, cols] = (2.0 * dot(gt_ref[...], u_ref[:, cols])).astype(BF16).T
 
         def grad_first(n):
             cols = slice(n, n + tile)

time: 208 us -> 207 us (level)
  no operation moved by 1% of the time
where the time goes in v5:
time: 207 us; the launch traced here: 206 us
  Pallas kernels  206 us (100%)
    pallas_call x1, Pallas kernels, train_step(): pl.pallas_call(functools.partial(gradient_kernel, 0.5 / (batch * width)),...  161 us
    pallas_call x1, Pallas kernels, train_step(): pl.pallas_call(functools.partial(update_kernel, LEARN_BASE / layers), in_...  44.7 us

profile of v5, /device:TPU:0, one launch (start us, length us, event | category | flops | bytes accessed | tf_op | source)
XLA Modules:
  0.0 206.5 jit_solution(1875558252726373670)
XLA Ops:
  0.6 0.0 copy-start.1
  0.6 0.0 copy-start
  0.7 161.1 %gradient.1 = (bf16[16,512,1024]{2,1,0:T(8,128)(2,1)S(1)}, bf16[14,256,1024]{2,1,0:T(8,128)(2,1)}, bf16[14,1024,256]{2,1,0:T(8,128)(2,1)}, bf16[14,1024,256]{2,1,0:T(8,128)(2,1)}) custom-call(bf16[1024,256]{1,0:T(8,128)(2,1)} %x_ref.2, bf16[1024,256]{1,0:T(8,128)(2,1)} %y_ref.2, f32[16,256,1024]{2,1,0:T(8,128)} %w1_hbm.1, f32[16,1024,256]{2,1,0:T(8,128)} %w2_hbm.1), custom_call_target="tpu_custom_call" | custom-call | flops 60129542144 | bytes 80000000 | tf_op jit(solution)/shard_map/gradient/pallas_call | solution.py:341
  161.7 0.0 copy-done.1
  161.8 0.0 copy-done
  161.8 44.7 %update_forward_next.1 = (f32[16,256,1024]{2,1,0:T(8,128)}, f32[16,1024,256]{2,1,0:T(8,128)}, f32[16,256,1024]{2,1,0:T(8,128)}, f32[16,1024,256]{2,1,0:T(8,128)}...) custom-call(bf16[1024,256]{1,0:T(8,128)(2,1)S(1)} %copy-done, bf16[1024,256]{1,0:T(8,128)(2,1)S(1)} %copy-done.1, ...), custom_call_target="tpu_custom_call" | custom-call | flops 17179869184 | bytes 160000000 | tf_op jit(solution)/shard_map/update_forward_next/pallas_call | solution.py:376
Async XLA Ops:
  0.6 161.1 %copy-start.1 = (bf16[1024,256]{1,0:T(8,128)(2,1)S(1)}, bf16[1024,256]{1,0:T(8,128)(2,1)}, u32[]{:S(2)}) copy-start(bf16[1024,256]{1,0:T(8,128)(2,1)} %y_ref.3) | copy-start | bytes 1572868
  0.6 161.1 %copy-start = (bf16[1024,256]{1,0:T(8,128)(2,1)S(1)}, bf16[1024,256]{1,0:T(8,128)(2,1)}, u32[]{:S(2)}) copy-start(bf16[1024,256]{1,0:T(8,128)(2,1)} %x_ref.3) | copy-start | bytes 1572868

commit v6 on v5

--- a/solution.py
+++ b/solution.py
@@ -15,10 +15,10 @@
 MESH = pl.DeviceIdType.MESH
 F32 = jnp.float32
 BF16 = jnp.bfloat16
-BACK_LIMIT = 46 << 20
-UPDATE_LIMIT = 26 << 20
-
-LOADS = 3
+BACK_LIMIT = 39 << 20
+UPDATE_LIMIT = 31 << 20
+
+KEPT = 2
 LAGS = (0, 2, 4, 6, 7, 9, 11, 13, 15)
 RING = 6
 SLOTS = 5
@@ -53,58 +53,71 @@
         h_ref[r:r + chunk, :] = h_ref[r:r + chunk, :] + dot(u_ref[r:r + chunk, :], w2b_ref[...])
 
 
-def update_kernel(rate, x_ref, y_ref, w1_hbm, w2_hbm, m1_hbm, m2_hbm, gr_ref,
+def update_kernel(rate, x_hbm, y_hbm, w1_hbm, w2_hbm, m1_hbm, m2_hbm, k1_ref, k2_ref, gr_ref,
                   w1o_hbm, w2o_hbm, m1o_hbm, m2o_hbm, loss_ref, h_ref,
-                  w1_ref, w2_ref, m1_ref, m2_ref, w1b_ref, w2b_ref, u_ref, in_sem, out_sem):
+                  w1_ref, w2_ref, m1_ref, m2_ref, w1b_ref, w2b_ref, u_ref, x_ref, y_ref, in_sem, out_sem, row_sem):
     layers, width = w1_hbm.shape[0], w1_hbm.shape[1]
     states = ((w1_hbm, w1_ref, w1o_hbm), (w2_hbm, w2_ref, w2o_hbm), (m1_hbm, m1_ref, m1o_hbm), (m2_hbm, m2_ref, m2o_hbm))
 
     def reads(layer):
         slot = layer % SLOTS
-        pairs = [(src, buf) for src, buf, _ in states]
-        return [pltpu.make_async_copy(src.at[layer], buf.at[slot], in_sem.at[slot, n]) for n, (src, buf) in enumerate(pairs)]
+        return [pltpu.make_async_copy(src.at[layer], buf.at[slot], in_sem.at[slot, n])
+                for n, (src, buf, _) in enumerate(states)]
 
     def writes(layer):
         slot = layer % SLOTS
         return [pltpu.make_async_copy(buf.at[slot], dst.at[layer], out_sem.at[slot, n])
                 for n, (_, buf, dst) in enumerate(states)]
 
-    for layer in range(AHEAD):
+    def refill(layer):
+        for copy in writes(layer - SLOTS):
+            copy.wait()
         for copy in reads(layer):
             copy.start()
-    h_ref[...] = x_ref[...].astype(F32)
-
-    @pl.loop(0, layers)
-    def _(layer):
+
+    def advance(layer, w1_old, w2_old, m1_old, m2_old):
         slot = layer % SLOTS
-
-        @pl.when(layer + AHEAD < layers)
-        def _():
-            @pl.when(layer + AHEAD >= SLOTS)
-            def _():
-                for copy in writes(layer + AHEAD - SLOTS):
-                    copy.wait()
-            for copy in reads(layer + AHEAD):
-                copy.start()
-
-        for copy in reads(layer):
-            copy.wait()
-        mom = MOMENTUM * m1_ref[slot] + gr_ref[layer, :width, :].astype(F32)
+        mom = MOMENTUM * m1_old[...] + gr_ref[layer, :width, :].astype(F32)
         m1_ref[slot] = mom
-        new = w1_ref[slot] - rate * mom
+        new = w1_old[...] - rate * mom
         w1_ref[slot] = new
         w1b_ref[...] = (0.5 * new).astype(BF16)
         for n in range(0, w2_ref.shape[1], width):
             part = slice(n, n + width)
-            mom = MOMENTUM * m2_ref[slot, part, :] + gr_ref[layer, width:, part].astype(F32)
+            mom = MOMENTUM * m2_old[part, :] + gr_ref[layer, width:, part].astype(F32)
             m2_ref[slot, part, :] = mom
-            new = w2_ref[slot, part, :] - rate * mom
+            new = w2_old[part, :] - rate * mom
             w2_ref[slot, part, :] = new
             w2b_ref[part, :] = new.astype(BF16)
         for copy in writes(layer):
             copy.start()
         layer_forward(h_ref, w1b_ref, w2b_ref, u_ref, None, 512, 256)
 
+    x_copy = pltpu.make_async_copy(x_hbm, x_ref, row_sem.at[0])
+    y_copy = pltpu.make_async_copy(y_hbm, y_ref, row_sem.at[1])
+    x_copy.start()
+    for layer in range(KEPT, SLOTS):
+        for copy in reads(layer):
+            copy.start()
+    y_copy.start()
+    x_copy.wait()
+    h_ref[...] = x_ref[...].astype(F32)
+    for layer in range(KEPT):
+        if layer + AHEAD >= SLOTS:
+            refill(layer + AHEAD)
+        advance(layer, *(ref.at[start + layer] for start in (0, KEPT) for ref in (k1_ref, k2_ref)))
+
+    @pl.loop(KEPT, layers)
+    def _(layer):
+        @pl.when(layer + AHEAD < layers)
+        def _():
+            refill(layer + AHEAD)
+
+        for copy in reads(layer):
+            copy.wait()
+        advance(layer, *(buf.at[layer % SLOTS] for _, buf, _ in states))
+
+    y_copy.wait()
     resid = h_ref[...] - y_ref[...].astype(F32)
     loss_ref[...] = jnp.sum((resid * resid).T, axis=0, keepdims=True) / (2 * width)
     for layer in range(layers - SLOTS, layers):
@@ -112,10 +125,11 @@
             copy.wait()
 
 
-def gradient_kernel(scale, x_ref, y_ref, w1f_hbm, w2f_hbm, sum_ref, w1_hbm, w2_hbm, hs_hbm,
-                    w1f_buf, w2f_buf, w1_buf, w2_buf, hs_buf, load_sem, save_sem, in_sem, g_ref, gb_ref, gt_ref, ht_ref, u_ref, q_ref,
+def gradient_kernel(scale, x_ref, y_ref, w1f_hbm, w2f_hbm, m1f_hbm, m2f_hbm,
+                    k1_ref, k2_ref, sum_ref, w1_hbm, w2_hbm, hs_hbm, w1_buf, w2_buf, hs_buf, load_sem, save_sem, in_sem, keep_sem, g_ref, gb_ref, gt_ref, ht_ref, u_ref, q_ref,
                     grad_ref, r0_ref, r1_ref, r2_ref, r3_ref, send_sem, recv_sem):
     layers = w1f_hbm.shape[0]
+    w1f_buf, m1f_buf, w2f_buf, m2f_buf = (ref.at[pl.ds(start, KEPT)] for ref in (k1_ref, k2_ref) for start in (0, KEPT))
     pod, data = lax.axis_index("pod"), lax.axis_index("data")
     z, y, x, c = pod // 2, pod % 2, data // 2, data % 2
     places = (x, y, z)
@@ -131,7 +145,7 @@
     saved = ((w1_hbm, w1_buf), (w2_hbm, w2_buf), (hs_hbm, hs_buf))
 
     def loads(layer):
-        slot = layer % LOADS
+        slot = layer % KEPT
         return [pltpu.make_async_copy(src.at[layer], buf.at[slot], load_sem.at[slot, n])
                 for n, (src, buf) in enumerate(((w1f_hbm, w1f_buf), (w2f_hbm, w2f_buf)))]
 
@@ -143,7 +157,10 @@
         slot = layer % 2
         return [pltpu.make_async_copy(src.at[layer], buf.at[slot], in_sem.at[slot, n]) for n, (src, buf) in enumerate(saved)]
 
-    for layer in range(LOADS - 1):
+    keeps = [pltpu.make_async_copy(src.at[pl.ds(0, KEPT)], buf, keep_sem.at[n]) for n, (src, buf) in enumerate(
+        ((w1f_hbm, w1f_buf), (w2f_hbm, w2f_buf), (m1f_hbm, m1f_buf), (m2f_hbm, m2f_buf)))]
+
+    for layer in range(KEPT - 1):
         for copy in loads(layer):
             copy.start()
     barrier = pltpu.get_barrier_semaphore()
@@ -155,9 +172,9 @@
     def _(layer):
         slot = layer % 2
 
-        @pl.when(layer + LOADS - 1 < layers)
-        def _():
-            for copy in loads(layer + LOADS - 1):
+        @pl.when(layer + KEPT - 1 < layers)
+        def _():
+            for copy in loads(layer + KEPT - 1):
                 copy.start()
 
         @pl.when(layer >= 2)
@@ -167,8 +184,8 @@
 
         for copy in loads(layer):
             copy.wait()
-        w1_buf[slot] = (0.5 * w1f_buf[layer % LOADS]).astype(BF16)
-        w2_buf[slot] = w2f_buf[layer % LOADS].astype(BF16)
+        w1_buf[slot] = (0.5 * w1f_buf[layer % KEPT]).astype(BF16)
+        w2_buf[slot] = w2f_buf[layer % KEPT].astype(BF16)
         layer_forward(g_ref, w1_buf.at[slot], w2_buf.at[slot], u_ref, hs_buf.at[slot], 1024, 256)
 
         @pl.when(layer < layers - 2)
@@ -177,6 +194,8 @@
                 copy.start()
 
     g_ref[...] = (g_ref[...] - y_ref[...].astype(F32)) * scale
+    for copy in keeps:
+        copy.start()
     pl.semaphore_wait(barrier, 4)
 
     def ring(slot):
@@ -323,6 +342,8 @@
             if taken[n] < 9:
                 step(taken[n], layers - 1 - n)
                 taken[n] += 1
+    for copy in keeps:
+        copy.wait()
 
 
 def solution(mesh):
@@ -338,21 +359,22 @@
         shape = jax.ShapeDtypeStruct
         matmul_flops = 2 * rows * width * hidden * layers
 
-        grads = pl.pallas_call(
+        kept = pl.pallas_call(
             functools.partial(gradient_kernel, 0.5 / (batch * width)),
-            in_specs=[pl.BlockSpec(memory_space=pltpu.VMEM)] * 2 + [pl.BlockSpec(memory_space=pl.ANY)] * 2,
-            out_specs=[pl.BlockSpec(memory_space=pltpu.VMEM)] + [pl.BlockSpec(memory_space=pl.ANY)] * 3,
-            out_shape=[pltpu.VMEM((layers, 2 * width, hidden), BF16), shape((layers - 2, width, hidden), BF16),
+            in_specs=[pl.BlockSpec(memory_space=pltpu.VMEM)] * 2 + [pl.BlockSpec(memory_space=pl.ANY)] * 4,
+            out_specs=[pl.BlockSpec(memory_space=pltpu.VMEM)] * 3 + [pl.BlockSpec(memory_space=pl.ANY)] * 3,
+            out_shape=[pltpu.VMEM((2 * KEPT, width, hidden), F32), pltpu.VMEM((2 * KEPT, hidden, width), F32),
+                       pltpu.VMEM((layers, 2 * width, hidden), BF16),
+                       shape((layers - 2, width, hidden), BF16),
                        shape((layers - 2, hidden, width), BF16), shape((layers - 2, rows, width), BF16)],
             scratch_shapes=[
-                pltpu.VMEM((LOADS, width, hidden), F32),
-                pltpu.VMEM((LOADS, hidden, width), F32),
                 pltpu.VMEM((2, width, hidden), BF16),
                 pltpu.VMEM((2, hidden, width), BF16),
                 pltpu.VMEM((2, rows, width), BF16),
-                pltpu.SemaphoreType.DMA((LOADS, 2)),
+                pltpu.SemaphoreType.DMA((KEPT, 2)),
                 pltpu.SemaphoreType.DMA((2, 3)),
                 pltpu.SemaphoreType.DMA((2, 3)),
+                pltpu.SemaphoreType.DMA((4,)),
                 pltpu.VMEM((rows, width), F32),
                 pltpu.VMEM((rows, width), BF16),
                 pltpu.VMEM((width, rows), BF16),
@@ -371,12 +393,12 @@
                                                  collective_id=0, has_side_effects=True),
             cost_estimate=pl.CostEstimate(flops=7 * matmul_flops, bytes_accessed=80_000_000, transcendentals=0),
             name="gradient",
-        )(x_now, y_now, w_first, w_second)[0]
+        )(x_now, y_now, w_first, w_second, m_first, m_second)[:3]
 
         outs = pl.pallas_call(
             functools.partial(update_kernel, LEARN_BASE / layers),
-            in_specs=[pl.BlockSpec(memory_space=pltpu.VMEM)] * 2 + [pl.BlockSpec(memory_space=pl.ANY)] * 4 +
-                     [pl.BlockSpec(memory_space=pltpu.VMEM)],
+            in_specs=[pl.BlockSpec(memory_space=pl.ANY)] * 6 +
+                     [pl.BlockSpec(memory_space=pltpu.VMEM)] * 3,
             out_specs=[pl.BlockSpec(memory_space=pl.ANY)] * 4 + [pl.BlockSpec(memory_space=pltpu.VMEM)] * 2,
             out_shape=[shape((layers, width, hidden), F32), shape((layers, hidden, width), F32),
                        shape((layers, width, hidden), F32), shape((layers, hidden, width), F32),
@@ -385,11 +407,14 @@
                             pltpu.VMEM((SLOTS, width, hidden), F32), pltpu.VMEM((SLOTS, hidden, width), F32),
                             pltpu.VMEM((width, hidden), BF16), pltpu.VMEM((hidden, width), BF16),
                             pltpu.VMEM((rows, hidden), BF16),
-                            pltpu.SemaphoreType.DMA((SLOTS, 4)), pltpu.SemaphoreType.DMA((SLOTS, 4))],
+                            pltpu.VMEM((rows, width), BF16), pltpu.VMEM((rows, width), BF16),
+                            pltpu.SemaphoreType.DMA((SLOTS, 4)), pltpu.SemaphoreType.DMA((SLOTS, 4)),
+                            pltpu.SemaphoreType.DMA((2,))],
             compiler_params=pltpu.CompilerParams(vmem_limit_bytes=UPDATE_LIMIT),
             cost_estimate=pl.CostEstimate(flops=2 * matmul_flops, bytes_accessed=160_000_000, transcendentals=0),
             name="update_forward_next",
-        )(x_next, y_next, w_first, w_second, m_first, m_second, pltpu.with_memory_space_constraint(grads, pltpu.VMEM))
+        )(*(pltpu.with_memory_space_constraint(a, pltpu.HBM) for a in (x_next, y_next)), w_first, w_second, m_first, m_second,
+          *(pltpu.with_memory_space_constraint(a, pltpu.VMEM) for a in kept))
         return outs[0], outs[1], outs[2], outs[3], outs[4].reshape(rows), outs[5]
 
     return jax.shard_map(train_step, mesh=mesh,

time: 207 us -> 207 us (level)
  no operation moved by 1% of the time
where the time goes in v6:
time: 207 us
  Pallas kernels  206 us (100%)
    pallas_call x1, Pallas kernels, train_step(): pl.pallas_call(functools.partial(gradient_kernel, 0.5 / (batch * width)),...  161 us
    pallas_call x1, Pallas kernels, train_step(): pl.pallas_call(functools.partial(update_kernel, LEARN_BASE / layers), in_...  44.8 us

profile of v6, /device:TPU:0, one launch (start us, length us, event | category | flops | bytes accessed | tf_op | source)
XLA Modules:
  0.0 206.7 jit_solution(14644860953285293359)
XLA Ops:
  0.6 161.0 %gradient.1 = (f32[4,256,1024]{2,1,0:T(8,128)S(1)}, f32[4,1024,256]{2,1,0:T(8,128)S(1)}, bf16[16,512,1024]{2,1,0:T(8,128)(2,1)S(1)}, bf16[14,256,1024]{2,1,0:T(8...) custom-call(bf16[1024,256]{1,0:T(8,128)(2,1)} %x_ref.1, bf16[1024,256]{1,0:T(8,128)(2,1)} %y_ref.1, ...), custom_call_target="tpu_custom_call" | custom-call | flops 60129542144 | bytes 80000000 | tf_op jit(solution)/shard_map/gradient/pallas_call | solution.py:362
  161.7 44.8 %update_forward_next.1 = (f32[16,256,1024]{2,1,0:T(8,128)}, f32[16,1024,256]{2,1,0:T(8,128)}, f32[16,256,1024]{2,1,0:T(8,128)}, f32[16,1024,256]{2,1,0:T(8,128)}...) custom-call(bf16[1024,256]{1,0:T(8,128)(2,1)} %x_hbm.1, bf16[1024,256]{1,0:T(8,128)(2,1)} %y_hbm.1, f32[16,256,1024]{2,1,0:T(8,128)} %w1_hbm.1, ...), custom_call_target="tpu_custom_call" | custom-call | flops 17179869184 | bytes 160000000 | tf_op jit(solution)/shard_map/update_forward_next/pallas_call | solution.py:398

commit v7 on v5

--- a/solution.py
+++ b/solution.py
@@ -16,13 +16,13 @@
 F32 = jnp.float32
 BF16 = jnp.bfloat16
 BACK_LIMIT = 46 << 20
-UPDATE_LIMIT = 26 << 20
+UPDATE_LIMIT = 30 << 20
 
 LOADS = 3
 LAGS = (0, 2, 4, 6, 7, 9, 11, 13, 15)
 RING = 6
-SLOTS = 5
-AHEAD = 3
+SLOTS = 6
+AHEAD = 4
 
 
 def dot(a, b, ca=1, cb=0):
@@ -103,7 +103,7 @@
             w2b_ref[part, :] = new.astype(BF16)
         for copy in writes(layer):
             copy.start()
-        layer_forward(h_ref, w1b_ref, w2b_ref, u_ref, None, 512, 256)
+        layer_forward(h_ref, w1b_ref, w2b_ref, u_ref, None, 1024, 256)
 
     resid = h_ref[...] - y_ref[...].astype(F32)
     loss_ref[...] = jnp.sum((resid * resid).T, axis=0, keepdims=True) / (2 * width)

time: 207 us -> 208 us (level)
  no operation moved by 1% of the time
where the time goes in v7:
time: 208 us
  Pallas kernels  207 us (100%)
    pallas_call x1, Pallas kernels, train_step(): pl.pallas_call(functools.partial(gradient_kernel, 0.5 / (batch * width)),...  161 us
    pallas_call x1, Pallas kernels, train_step(): pl.pallas_call(functools.partial(update_kernel, LEARN_BASE / layers), in_...  46 us

profile of v7, /device:TPU:0, one launch (start us, length us, event | category | flops | bytes accessed | tf_op | source)
XLA Modules:
  0.0 207.8 jit_solution(14574343300094650721)
XLA Ops:
  0.6 0.0 copy-start.1
  0.6 0.0 copy-start
  0.7 161.1 %gradient.1 = (bf16[16,512,1024]{2,1,0:T(8,128)(2,1)S(1)}, bf16[14,256,1024]{2,1,0:T(8,128)(2,1)}, bf16[14,1024,256]{2,1,0:T(8,128)(2,1)}, bf16[14,1024,256]{2,1,0:T(8,128)(2,1)}) custom-call(bf16[1024,256]{1,0:T(8,128)(2,1)} %x_ref.2, bf16[1024,256]{1,0:T(8,128)(2,1)} %y_ref.2, f32[16,256,1024]{2,1,0:T(8,128)} %w1_hbm.1, f32[16,1024,256]{2,1,0:T(8,128)} %w2_hbm.1), custom_call_target="tpu_custom_call" | custom-call | flops 60129542144 | bytes 80000000 | tf_op jit(solution)/shard_map/gradient/pallas_call | solution.py:341
  161.7 0.0 copy-done.1
  161.8 0.0 copy-done
  161.8 46.0 %update_forward_next.1 = (f32[16,256,1024]{2,1,0:T(8,128)}, f32[16,1024,256]{2,1,0:T(8,128)}, f32[16,256,1024]{2,1,0:T(8,128)}, f32[16,1024,256]{2,1,0:T(8,128)}...) custom-call(bf16[1024,256]{1,0:T(8,128)(2,1)S(1)} %copy-done, bf16[1024,256]{1,0:T(8,128)(2,1)S(1)} %copy-done.1, ...), custom_call_target="tpu_custom_call" | custom-call | flops 17179869184 | bytes 160000000 | tf_op jit(solution)/shard_map/update_forward_next/pallas_call | solution.py:376
Async XLA Ops:
  0.6 161.1 %copy-start.1 = (bf16[1024,256]{1,0:T(8,128)(2,1)S(1)}, bf16[1024,256]{1,0:T(8,128)(2,1)}, u32[]{:S(2)}) copy-start(bf16[1024,256]{1,0:T(8,128)(2,1)} %y_ref.3) | copy-start | bytes 1572868
  0.6 161.1 %copy-start = (bf16[1024,256]{1,0:T(8,128)(2,1)S(1)}, bf16[1024,256]{1,0:T(8,128)(2,1)}, u32[]{:S(2)}) copy-start(bf16[1024,256]{1,0:T(8,128)(2,1)} %x_ref.3) | copy-start | bytes 1572868

commit v8 on v5

--- a/solution.py
+++ b/solution.py
@@ -102,7 +102,7 @@
             w2_ref[slot, part, :] = new
             w2b_ref[part, :] = new.astype(BF16)
         for copy in writes(layer):
-            copy.start()
+            copy.start(priority=1)
         layer_forward(h_ref, w1b_ref, w2b_ref, u_ref, None, 512, 256)
 
     resid = h_ref[...] - y_ref[...].astype(F32)

time: 207 us -> 207 us (level)
  no operation moved by 1% of the time
where the time goes in v8:
time: 207 us
  Pallas kernels  206 us (100%)
    pallas_call x1, Pallas kernels, train_step(): pl.pallas_call(functools.partial(gradient_kernel, 0.5 / (batch * width)),...  161 us
    pallas_call x1, Pallas kernels, train_step(): pl.pallas_call(functools.partial(update_kernel, LEARN_BASE / layers), in_...  45.2 us

profile of v8, /device:TPU:0, one launch (start us, length us, event | category | flops | bytes accessed | tf_op | source)
XLA Modules:
  0.0 207.0 jit_solution(15696077796288688794)
XLA Ops:
  0.6 0.0 copy-start.1
  0.6 0.0 copy-start
  0.7 161.1 %gradient.1 = (bf16[16,512,1024]{2,1,0:T(8,128)(2,1)S(1)}, bf16[14,256,1024]{2,1,0:T(8,128)(2,1)}, bf16[14,1024,256]{2,1,0:T(8,128)(2,1)}, bf16[14,1024,256]{2,1,0:T(8,128)(2,1)}) custom-call(bf16[1024,256]{1,0:T(8,128)(2,1)} %x_ref.2, bf16[1024,256]{1,0:T(8,128)(2,1)} %y_ref.2, f32[16,256,1024]{2,1,0:T(8,128)} %w1_hbm.1, f32[16,1024,256]{2,1,0:T(8,128)} %w2_hbm.1), custom_call_target="tpu_custom_call" | custom-call | flops 60129542144 | bytes 80000000 | tf_op jit(solution)/shard_map/gradient/pallas_call | solution.py:341
  161.7 0.0 copy-done.1
  161.8 0.0 copy-done
  161.8 45.2 %update_forward_next.1 = (f32[16,256,1024]{2,1,0:T(8,128)}, f32[16,1024,256]{2,1,0:T(8,128)}, f32[16,256,1024]{2,1,0:T(8,128)}, f32[16,1024,256]{2,1,0:T(8,128)}...) custom-call(bf16[1024,256]{1,0:T(8,128)(2,1)S(1)} %copy-done, bf16[1024,256]{1,0:T(8,128)(2,1)S(1)} %copy-done.1, ...), custom_call_target="tpu_custom_call" | custom-call | flops 17179869184 | bytes 160000000 | tf_op jit(solution)/shard_map/update_forward_next/pallas_call | solution.py:376
Async XLA Ops:
  0.6 161.1 %copy-start.1 = (bf16[1024,256]{1,0:T(8,128)(2,1)S(1)}, bf16[1024,256]{1,0:T(8,128)(2,1)}, u32[]{:S(2)}) copy-start(bf16[1024,256]{1,0:T(8,128)(2,1)} %y_ref.3) | copy-start | bytes 1572868
  0.6 161.1 %copy-start = (bf16[1024,256]{1,0:T(8,128)(2,1)S(1)}, bf16[1024,256]{1,0:T(8,128)(2,1)}, u32[]{:S(2)}) copy-start(bf16[1024,256]{1,0:T(8,128)(2,1)} %x_ref.3) | copy-start | bytes 1572868
